TPU v7x, 128 devices: a whole 4x4x4 slice. The times are simulated.
128 devices in a mesh: batch: 32 (over y, z, core), mp: 4 (over x).
Axes of the slice: x: 4, y: 4, z: 4, core: 2. Of those that a mesh axis runs over, the one named last changes fastest.
Arguments:
- init_state: float32 [16384, 256], P(('batch', 'mp')), may hold values from -6 to 6
- brownian: bfloat16 [32, 16384, 256], P(None, ('batch', 'mp')), may hold values from -6 to 6
- step_size: float32 [16384], P(('batch', 'mp')), may hold values from 0.02 to 0.1
- lengths: int32 [16384], P(('batch', 'mp')), may hold values from 1 to 32, as said below
- obs_steps: int32 [16384, 8], P(('batch', 'mp')), may hold values from 1 to 32, as said below
- observed: bfloat16 [16384, 8, 128], P(('batch', 'mp')), may hold values from -6 to 6
- w_in: bfloat16 [256, 1024], P(None, 'mp'), may hold values from -0.375 to 0.375
- b_in: bfloat16 [1024], P('mp'), may hold values from -3 to 3
- w_out: bfloat16 [1024, 256], P('mp'), may hold values from -0.1875 to 0.1875
- b_out: float32 [256], replicated, may hold values from -4 to 4
- decoder: bfloat16 [256, 128], replicated, may hold values from -0.375 to 0.375
- prior_rate: float32 [256], replicated, may hold values from 0.1 to 2
- diffusion: float32 [256], replicated, may hold values from 0.7 to 1.4
Outputs:
- elbo_series: float32 [16384], P(('batch', 'mp'))
- scores: float32 [2], replicated
- grad_w_in: float32 [256, 1024], P(None, 'mp')
- grad_b_in: float32 [1024], P('mp')
- grad_w_out: float32 [1024, 256], P('mp')
- grad_b_out: float32 [256], replicated
- grad_decoder: float32 [256, 128], replicated
- grad_init: float32 [16384, 256], P(('batch', 'mp'))
Inputs may be any that keep to these rules, and one draw needn't show every extreme that they name: `lengths`: some series has 32 live steps in every draw. obs_steps[i, j] is at most lengths[i].
All inputs are finite; a program needn't handle non-finite values.
Results may differ from a plain program's by a relative error of at most 0.0019.
Values may be sent and summed in bfloat16 or wider, within the bound.
A program may use at most 64 MiB of HBM per device.

v0:
```python
import functools

import jax
import jax.numpy as jnp
from jax import lax
from jax.sharding import Mesh
from jax.sharding import PartitionSpec as P

BATCH_MP = ("batch_0", "batch_1", "batch_2", "mp")
BATCH = ("batch_0", "batch_1", "batch_2")


def turned_gather(arrays, axis, dims):
    turned = [jnp.moveaxis(a, dim, 0) for a, dim in zip(arrays, dims)]
    widths = [t[0].size for t in turned]
    both = jnp.concatenate([t.reshape(-1, w) for t, w in zip(turned, widths)], axis=1)
    whole = lax.all_gather(both, axis, axis=0, tiled=True)
    blocks = jnp.split(whole, [sum(widths[:k]) for k in range(1, len(widths))], axis=1)
    return tuple(
        (
            jnp.moveaxis(b.reshape(-1, *t.shape[1:]), 0, dim)
            for b, t, dim in zip(blocks, turned, dims)
        )
    )


def by_axis(shard, axes):
    return functools.reduce(lax.psum, axes, shard)


def solve(
    init_state,
    brownian,
    step_size,
    lengths,
    obs_steps,
    observed,
    horizon,
    w_in_all,
    b_in_all,
    w_out_all,
    b_out,
    decoder,
    prior_rate,
    diffusion,
):
    row_count = init_state.shape[0]
    num_steps = brownian.shape[0]
    latent_width = init_state.shape[1]
    hidden_width = w_in_all.shape[1]
    step_col = step_size[:, None]
    root_col = jnp.sqrt(step_size)[:, None]
    bias_in = b_in_all.astype(jnp.float32)

    def forward(step_index, loop_state):
        trajectory, activities, residuals, kl_sum = loop_state
        current = lax.dynamic_index_in_dim(trajectory, step_index, 0, keepdims=False)
        increment = lax.dynamic_index_in_dim(brownian, step_index, 0, keepdims=False)
        live_now = (step_index < lengths).astype(jnp.float32)
        activity = jnp.tanh(
            jnp.dot(current.astype(jnp.bfloat16), w_in_all, preferred_element_type=jnp.float32)
            + bias_in
        ).astype(jnp.bfloat16)
        drift_now = jnp.dot(activity, w_out_all, preferred_element_type=jnp.float32) + b_out
        residual = (drift_now + prior_rate * current) / diffusion
        kl_sum = kl_sum + live_now * 0.5 * step_size * jnp.sum(residual * residual, axis=1)
        following = current + live_now[:, None] * (
            step_col * drift_now + diffusion * root_col * increment.astype(jnp.float32)
        )
        trajectory = lax.dynamic_update_index_in_dim(trajectory, following, step_index + 1, 0)
        activities = lax.dynamic_update_index_in_dim(activities, activity, step_index, 0)
        residuals = lax.dynamic_update_index_in_dim(residuals, residual, step_index, 0)
        return (trajectory, activities, residuals, kl_sum)

    start_path = lax.dynamic_update_index_in_dim(
        jnp.zeros((num_steps + 1, row_count, latent_width), jnp.float32), init_state, 0, 0
    )
    start_forward = (
        start_path,
        jnp.zeros((num_steps, row_count, hidden_width), jnp.bfloat16),
        jnp.zeros((num_steps, row_count, latent_width), jnp.float32),
        jnp.zeros((row_count,), jnp.float32),
    )
    trajectory, activities, residuals, kl_total = lax.fori_loop(0, horizon, forward, start_forward)
    picked = trajectory[obs_steps, jnp.arange(row_count, dtype=jnp.int32)[:, None]]
    picked_round = picked.astype(jnp.bfloat16).reshape(-1, latent_width)
    flat_obs = observed.reshape(-1, observed.shape[2]).astype(jnp.float32)
    misfit = jnp.dot(picked_round, decoder, preferred_element_type=jnp.float32) - flat_obs
    loglik = -0.5 * jnp.sum((misfit * misfit).reshape(row_count, -1), axis=1)
    misfit_round = misfit.astype(jnp.bfloat16)
    decoder_grad = jnp.dot(picked_round.T, misfit_round, preferred_element_type=jnp.float32)
    misfit_back = jnp.dot(misfit_round, decoder.T, preferred_element_type=jnp.float32).reshape(
        row_count, obs_steps.shape[1], latent_width
    )
    onehot = (
        obs_steps[:, :, None] == jnp.arange(num_steps + 1, dtype=jnp.int32)[None, None, :]
    ).astype(jnp.float32)
    obs_back = jnp.einsum("bjs,bjl->sbl", onehot, misfit_back, precision=lax.Precision.HIGHEST)

    def backward(back_index, loop_state):
        cotangent, sum_w_in, sum_b_in, sum_w_out, sum_b_out = loop_state
        step_index = horizon - 1 - back_index
        current = lax.dynamic_index_in_dim(trajectory, step_index, 0, keepdims=False)
        activity = lax.dynamic_index_in_dim(activities, step_index, 0, keepdims=False)
        residual = lax.dynamic_index_in_dim(residuals, step_index, 0, keepdims=False)
        obs_here = lax.dynamic_index_in_dim(obs_back, step_index, 0, keepdims=False)
        live_now = (step_index < lengths).astype(jnp.float32)
        factor = (live_now * step_size)[:, None]
        scaled = residual / diffusion
        update = factor * (cotangent + scaled)
        update_round = update.astype(jnp.bfloat16)
        activity_value = activity.astype(jnp.float32)
        pre_grad = jnp.dot(update_round, w_out_all.T, preferred_element_type=jnp.float32) * (
            1.0 - activity_value * activity_value
        )
        pre_round = pre_grad.astype(jnp.bfloat16)
        cotangent = (
            cotangent
            + factor * prior_rate * scaled
            + jnp.dot(pre_round, w_in_all.T, preferred_element_type=jnp.float32)
            + obs_here
        )
        sum_w_in = sum_w_in + jnp.dot(
            current.astype(jnp.bfloat16).T, pre_round, preferred_element_type=jnp.float32
        )
        sum_b_in = sum_b_in + jnp.sum(pre_grad, axis=0)
        sum_w_out = sum_w_out + jnp.dot(
            activity.T, update_round, preferred_element_type=jnp.float32
        )
        sum_b_out = sum_b_out + jnp.sum(update, axis=0)
        return (cotangent, sum_w_in, sum_b_in, sum_w_out, sum_b_out)

    start_back = (
        lax.dynamic_index_in_dim(obs_back, horizon, 0, keepdims=False),
        jnp.zeros((latent_width, hidden_width), jnp.float32),
        jnp.zeros((hidden_width,), jnp.float32),
        jnp.zeros((hidden_width, latent_width), jnp.float32),
        jnp.zeros((latent_width,), jnp.float32),
    )
    cotangent, sum_w_in, sum_b_in, sum_w_out, sum_b_out = lax.fori_loop(
        0, horizon, backward, start_back
    )
    divisor = (latent_width * lengths + observed.shape[2] * obs_steps.shape[1]).astype(jnp.float32)
    elbo_rows = (loglik - kl_total) / divisor
    return (
        elbo_rows,
        cotangent,
        jnp.sum(loglik),
        jnp.sum(kl_total),
        sum_w_in,
        sum_b_in,
        sum_w_out,
        sum_b_out,
        decoder_grad,
    )


def on_device(
    init_state,
    brownian,
    step_size,
    lengths,
    obs_steps,
    observed,
    w_in,
    b_in,
    w_out,
    b_out,
    decoder,
    prior_rate,
    diffusion,
):
    w_in_all, w_out_all, b_in_all = turned_gather((w_in, w_out, b_in), "mp", (1, 0, 0))
    row_count = init_state.shape[0]
    num_steps = brownian.shape[0]
    hidden_width = w_in_all.shape[1]
    shared = (w_in_all, b_in_all, w_out_all, b_out, decoder, prior_rate, diffusion)
    outcome = solve(
        init_state, brownian, step_size, lengths, obs_steps, observed, num_steps, *shared
    )
    (
        elbo_series,
        cotangent,
        loglik_local,
        kl_local,
        sum_w_in,
        sum_b_in,
        sum_w_out,
        sum_b_out,
        decoder_grad,
    ) = outcome
    loglik_all, kl_all = (by_axis(loglik_local, BATCH_MP), by_axis(kl_local, BATCH_MP))
    total_series = row_count * lax.axis_size(BATCH) * lax.axis_size("mp")
    share = hidden_width // lax.axis_size("mp")
    offset = lax.axis_index("mp") * share
    all_w_in, all_b_in, all_w_out, all_b_out, all_decoder = lax.psum(
        (sum_w_in, sum_b_in, sum_w_out, sum_b_out, decoder_grad), BATCH_MP
    )
    own_w_in = lax.dynamic_slice_in_dim(all_w_in, offset, share, 1)
    own_b_in = lax.dynamic_slice_in_dim(all_b_in, offset, share, 0)
    own_w_out = lax.dynamic_slice_in_dim(all_w_out, offset, share, 0)
    scores = jnp.stack([loglik_all / total_series, kl_all / total_series])
    return (
        elbo_series,
        scores,
        own_w_in / total_series,
        own_b_in / total_series,
        own_w_out / total_series,
        all_b_out / total_series,
        all_decoder / total_series,
        cotangent,
    )


def solution(mesh):
    torus = Mesh(
        mesh.devices.reshape(4, 4, 2, mesh.shape["mp"]), ("batch_0", "batch_1", "batch_2", "mp")
    )
    placed = (
        P(BATCH_MP, None),
        P(None, BATCH_MP, None),
        P(BATCH_MP),
        P(BATCH_MP),
        P(BATCH_MP, None),
        P(BATCH_MP, None, None),
        P(None, "mp"),
        P("mp"),
        P("mp", None),
        P(),
        P(),
        P(),
        P(),
    )
    return jax.shard_map(
        on_device,
        mesh=torus,
        in_specs=placed,
        out_specs=(
            P(BATCH_MP),
            P(),
            P(None, "mp"),
            P("mp"),
            P("mp", None),
            P(),
            P(),
            P(BATCH_MP, None),
        ),
        check_vma=False,
    )
```

profile of v0, /device:TPU:1, one launch (start us, length us, event | category | flops | bytes accessed | tf_op | source)
XLA Modules:
  0.0 789.1 jit_solution(2459899260719976224)
XLA Ops:
  14.5 3.5 dynamic_update_slice.37
  18.0 19.7 %all-gather.2.cloned.1.call-done = bf16[1024,513]{1,0:T(8,128)(2,1)} async-done(((bf16[256,513]{1,0:T(8,128)(2,1)}), bf16[1024,513]{1,0:T(8,128)(2,1)}) %all-gather.2.cloned.1.call-update) | async-done | bytes 1050640 | tf_op jit(solution)/shard_map/all_gather | solution.py:17
  37.7 2.3 fusion.37
  42.4 313.4 %while.46 = (s32[]{:T(128)}, f32[33,128,256]{2,1,0:T(8,128)}, bf16[32,128,1024]{2,1,0:T(8,128)(2,1)}, f32[32,128,256]{2,1,0:T(8,128)}, f32[128]{0:T(128)S(1)}, /...) while((s32[]{:T(128)}, f32[33,128,256]{2,1,0:T(8,128)}, ...), condition=%wide.region_2.3_spmd.clone, body=%wide.region_0.2_spmd.clone.sunk | while | flops 135005056 | bytes 20398324 | solution.py:84
  45.2 2.2 copy.44
  55.0 2.2 copy.44
  64.8 2.2 copy.44
  74.6 2.2 copy.44
  84.4 2.2 copy.44
  94.2 2.2 copy.44
  104.0 2.2 copy.44
  113.7 2.2 copy.44
  123.6 2.2 copy.44
  133.3 2.2 copy.44
  143.1 2.2 copy.44
  152.9 2.2 copy.44
  162.7 2.2 copy.44
  172.5 2.2 copy.44
  182.3 2.2 copy.44
  192.1 2.2 copy.44
  201.9 2.2 copy.44
  355.8 3.9 convert.37
  359.7 12.4 %gather_fusion = bf16[1024,256]{1,0:T(8,128)(2,1)S(1)} fusion(f32[33,128,256]{2,1,0:T(8,128)} %get-tuple-element.970, s32[1024]{0:T(1024)S(1)} %reshape.71), kind=kCustom, calls=%fused_computation | custom fusion | bytes 1056768 | tf_op jit(solution)/shard_map/gather | solution.py:85
  374.8 2.9 fusion.23
  377.8 2.3 copy-done.3
  380.1 242.8 %while.47 = (s32[]{:T(128)}, f32[128,256]{1,0:T(8,128)S(1)}, f32[256,1024]{1,0:T(8,128)S(1)}, f32[1024]{0:T(1024)S(1)}, f32[1024,256]{1,0:T(8,128)S(1)}, /*index...) while((s32[]{:T(128)}, f32[128,256]{1,0:T(8,128)S(1)}, ...), condition=%wide.region_18.19_spmd.clone, body=%wide.region_15.18_spmd.clone.sunk | while | flops 270632448 | bytes 9987913 | solution.py:140
  625.5 9.0 %all-reduce.5 = (f32[]{:T(128)}, f32[]{:T(128)}) all-reduce(f32[]{:T(128)} %get-tuple-element.1030, f32[]{:T(128)} %get-tuple-element.1028), channel_id=1, replica_groups=mesh['batch_0'=4,'batch_1'=4,'batch_2'=2,'mp'=4] {'batch_0'}, use_global_device_ids=true, to_apply=%region_11.12 | all-reduce | flops 2 | bytes 16 | tf_op jit(solution)/shard_map/psum | solution.py:28
  634.5 9.2 %all-reduce.4 = (f32[]{:T(128)}, f32[]{:T(128)}) all-reduce(f32[]{:T(128)} %get-tuple-element.1012, f32[]{:T(128)} %get-tuple-element.1013), channel_id=1, replica_groups=mesh['batch_0'=4,'batch_1'=4,'batch_2'=2,'mp'=4] {'batch_1'}, use_global_device_ids=true, to_apply=%region_12.13 | all-reduce | flops 2 | bytes 16 | tf_op jit(solution)/shard_map/psum | solution.py:28
  643.7 9.0 %all-reduce.6 = (f32[]{:T(128)}, f32[]{:T(128)}) all-reduce(f32[]{:T(128)} %get-tuple-element.1010, f32[]{:T(128)} %get-tuple-element.1011), channel_id=1, replica_groups=mesh['batch_0'=4,'batch_1'=4,'batch_2'=2,'mp'=4] {'batch_2'}, use_global_device_ids=true, to_apply=%region_13.14 | all-reduce | flops 2 | bytes 16 | tf_op jit(solution)/shard_map/psum | solution.py:28
  652.6 8.3 %all-reduce.3 = (f32[]{:T(128)}, f32[]{:T(128)}) all-reduce(f32[]{:T(128)} %get-tuple-element.1014, f32[]{:T(128)} %get-tuple-element.1015), channel_id=1, replica_groups=mesh['batch_0'=4,'batch_1'=4,'batch_2'=2,'mp'=4] {'mp'}, use_global_device_ids=true, to_apply=%region_14.15 | all-reduce | flops 2 | bytes 16 | tf_op jit(solution)/shard_map/psum | solution.py:28
  662.2 64.6 %all-reduce.1 = (f32[1024]{0:T(1024)S(1)}, f32[256]{0:T(256)S(1)}) all-reduce(f32[1024]{0:T(1024)S(1)} %get-tuple-element.769, f32[256]{0:T(256)S(1)} %get-tuple-element.771), channel_id=1, replica_groups=mesh['batch_0'=4,'batch_1'=4,'batch_2'=2,'mp'=4] {'batch_0','batch_1','b..., use_global_device_ids=true, to_apply=%region_20.21 | all-reduce | flops 1280 | bytes 10240 | tf_op jit(solution)/shard_map/psum | solution.py:196
  728.1 50.8 %all-reduce.9.cloned.1.call-done = (f32[256,1024]{1,0:T(8,128)}, f32[1024,256]{1,0:T(8,128)}, f32[256,128]{1,0:T(8,128)}) async-done(((f32[256,1024]{1,0:T(8,128)}, f32[1024,256]{1,0:T(8,128)}, f32[256,128]{1,0:T(8,128)}), (f32[256,1024]{1,0:T(8,128)}, f32[1024,256]{1,0:T(8,128)}, f32[256,128]{1,0:T(8,128)})) %all-reduce.9.cloned.1.call-update) | async-done | bytes 2228240 | tf_op jit(solution)/shard_map/psum | solution.py:196
  (645 shorter events, 534.1 us)
Async XLA Ops:
  7.2 364.9 %copy-start = (bf16[256,128]{1,0:T(8,128)(2,1)S(1)}, bf16[256,128]{1,0:T(8,128)(2,1)}, u32[]{:S(2)}) copy-start(bf16[256,128]{1,0:T(8,128)(2,1)} %param.27) | copy-start | bytes 196612
  7.2 10.8 %copy-start.8 = (f32[128]{0:T(128)S(1)}, f32[128]{0:T(128)}, u32[]{:S(2)}) copy-start(f32[128]{0:T(128)} %param.19) | copy-start | bytes 1540
  7.2 30.5 %all-gather.2.cloned.1.call-start = ((), (), s32[]{:S(2)}) async-start(), calls=%async_computation | async-start | bytes 1638400 | tf_op jit(solution)/shard_map/all_gather | solution.py:17
  10.7 768.1 %all-reduce.9.cloned.1.call-start = ((), (), s32[]{:S(2)}) async-start(), calls=%async_computation.1 | async-start | bytes 4456448 | tf_op jit(solution)/shard_map/psum | solution.py:196
  14.5 27.8 %copy-start.6 = (f32[256]{0:T(256)S(1)}, f32[256]{0:T(256)}, u32[]{:S(2)}) copy-start(f32[256]{0:T(256)} %param.29) | copy-start | bytes 3076
  14.5 27.8 %copy-start.7 = (s32[128]{0:T(128)S(1)}, s32[128]{0:T(128)}, u32[]{:S(2)}) copy-start(s32[128]{0:T(128)} %param.20) | copy-start | bytes 1540
  14.5 27.9 %copy-start.9 = (f32[256]{0:T(256)S(1)}, f32[256]{0:T(256)}, u32[]{:S(2)}) copy-start(f32[256]{0:T(256)} %param.28) | copy-start | bytes 3076
  14.5 27.9 %copy-start.10 = (f32[256]{0:T(256)S(1)}, f32[256]{0:T(256)}, u32[]{:S(2)}) copy-start(f32[256]{0:T(256)} %param.26) | copy-start | bytes 3076
  405.1 4.0 copy-start.5
  412.7 4.0 copy-start.5
  420.3 4.0 copy-start.5
  427.9 4.0 copy-start.5
  435.5 4.0 copy-start.5
  443.0 4.0 copy-start.5
  450.6 4.0 copy-start.5
  458.2 4.0 copy-start.5
  465.8 4.0 copy-start.5
  473.4 4.0 copy-start.5
  481.0 4.0 copy-start.5
  488.6 4.0 copy-start.5
  496.2 4.0 copy-start.5
  503.7 4.0 copy-start.5
  511.3 4.0 copy-start.5
  518.9 4.0 copy-start.5
  526.5 4.0 copy-start.5
  534.1 4.0 copy-start.5
  541.7 4.0 copy-start.5
  549.3 4.0 copy-start.5
  556.9 4.0 copy-start.5
  579.6 4.0 copy-start.5
  617.6 4.0 copy-start.5
  622.8 159.4 %copy-start.4 = (f32[128,256]{1,0:T(8,128)}, f32[128,256]{1,0:T(8,128)S(1)}, u32[]{:S(2)}) copy-start(f32[128,256]{1,0:T(8,128)S(1)} %get-tuple-element.763) | copy-start | bytes 393220
  (12 other events, 41.1 us)
Sparse Core Ops, SparseCore 0:
  10.8 26.8 all-gather.1
  624.3 154.5 all-reduce.8
where the time goes:
time: 799 us; the launch traced here: 789 us
  matrix products  284 us (36%)
  local copies, waits for them, and re-layouts  234 us (29%)
  blocking collectives  100 us (13%)
  other arithmetic  80.4 us (10%)
  waiting for transfers between devices  70.5 us (9%)
  between operations  15.6 us (2%)
    while x128, local copies, waits for them, and re-layouts  136 us
    psum x1, blocking collectives, on_device(): lax.psum((sum_w_in, sum_b_in, sum_w_out, sum_b_out, decoder_grad), BATCH_MP)  64.6 us
    dot_general x32, matrix products, forward(): jnp.dot(current.astype(jnp.bfloat16), w_in_all, preferred_element_type=jn...  59.4 us
    dot_general x32, matrix products, forward(): jnp.dot(activity, w_out_all, preferred_element_type=jnp.float32) + b_out  55.5 us
    psum x1, waiting for transfers between devices, on_device(): lax.psum((sum_w_in, sum_b_in, sum_w_out, sum_b_out, decoder_grad), BATCH_MP)  50.8 us
    dot_general x32, matrix products, backward(): jnp.dot(activity.T, update_round, preferred_element_type=jnp.float32)  44.8 us
    dynamic_slice x32, local copies, waits for them, and re-layouts, backward(): obs_here = lax.dynamic_index_in_dim(obs_back, step_index, 0, keepdims=False)  42.4 us
    dot_general x32, matrix products, backward(): jnp.dot(current.astype(jnp.bfloat16).T, pre_round, preferred_element_type...  41.2 us
  transfers between devices with their start and end apart: 2, of which 2 were waited for; matrix products, arithmetic and copies ran while one was open for 1% of the time, Pallas kernels for 0%

commit v1 on v0

v1 whole, which is shorter than its diff:
```python
import functools

import jax
import jax.numpy as jnp
from jax import lax
from jax.experimental import pallas as pl
from jax.experimental.pallas import tpu as pltpu
from jax.sharding import Mesh
from jax.sharding import PartitionSpec as P

BATCH_MP = ("batch_0", "batch_1", "batch_2", "mp")
F32, BF16 = jnp.float32, jnp.bfloat16
UNROLL = 2


def mm(a, b):
    return jnp.dot(a, b, preferred_element_type=F32)


def twice(a):
    return jnp.concatenate([a, a], axis=1)


def solve_kernel(
    scale,
    init, brown, step, length, obs, observed, w_in, b_in, w_out, b_out, dec, prior, diff,
    elbo, big, small, ginit,
    state, stepb, lenb, dr, obsb, obsf, acc, klacc, traj_t, acts, scaled, pre, back, upd_t,
    w_in_t, w_out_t, dec_t, cot, sum_in, sum_out,
):
    steps, rows, width = brown.shape
    hidden = w_in.shape[1]
    n_obs = obs.shape[1]

    stepb[...] = jnp.broadcast_to(step[...], (rows, rows)).T
    lenb[...] = jnp.broadcast_to(length[...], (rows, rows)).T
    dr[...] = diff[...] * twice(jnp.sqrt(stepb[...]))
    obs_all = obs[...]
    for j in range(n_obs):
        obsb[j] = jnp.broadcast_to(obs_all[:, j : j + 1], (rows, rows))
    obsf[...] = observed[...].astype(F32).reshape(rows * n_obs, dec.shape[1])
    w_in_t[...] = w_in[...].T
    w_out_t[...] = w_out[...].T
    dec_flip = dec[...].T
    dec_t[...] = jnp.concatenate([dec_flip, dec_flip], axis=0)
    klacc[...] = jnp.zeros_like(klacc)
    acc[...] = jnp.zeros_like(acc)
    sum_in[...] = jnp.zeros_like(sum_in)
    sum_out[...] = jnp.zeros_like(sum_out)
    state[...] = init[...]
    bias = b_in[...].astype(F32)
    inv = 1.0 / diff[...]

    def see(k, rounded):
        seen = mm(rounded, dec[...])
        for j in range(n_obs):
            acc[j] = jnp.where(obsb[j] == k, seen, acc[j])

    def at(k):
        return pl.ds(pl.multiple_of(k * rows, rows), rows)

    def forward(k, carry):
        s = state[...]
        rounded = s.astype(BF16)
        activity = jnp.tanh(mm(rounded, w_in[...]) + bias).astype(BF16)
        drift = mm(activity, w_out[...]) + b_out[...]
        live = lenb[...] > k
        factor = jnp.where(live, stepb[...], 0.0)
        residual = (drift + prior[...] * s) * inv
        noise = dr[...] * brown[k].astype(F32)
        state[...] = s + twice(factor) * drift + jnp.where(twice(live), noise, 0.0)
        acts[at(k), :] = activity
        scaled[k] = residual * inv
        square = residual * residual
        klacc[...] += (0.5 * factor) * (square[:, :rows] + square[:, rows:])
        traj_t[:, at(k)] = rounded.T
        see(k, rounded)
        return carry

    lax.fori_loop(0, steps, forward, 0, unroll=UNROLL)
    last = state[...].astype(BF16)
    traj_t[:, at(steps)] = last.T
    see(steps, last)

    total = jnp.zeros((rows, rows), F32)
    for j in range(n_obs):
        misfit = acc[j] - obsf[pl.ds(j, rows, stride=n_obs), :]
        total = total + misfit * misfit
        acc[j] = misfit.astype(BF16).astype(F32)
    loglik = -0.5 * total
    divisor = (width * lenb[...] + rows * n_obs).astype(F32)
    per_series = jnp.sum(loglik - klacc[...], axis=1, keepdims=True) / divisor
    elbo[...] = per_series.T[0:1, :]

    def gathered(k):
        m = jnp.zeros((rows, rows), F32)
        for j in range(n_obs):
            m = m + jnp.where(obsb[j] == k, acc[j], 0.0)
        high = m.astype(BF16)
        low = (m - high.astype(F32)).astype(BF16)
        return jnp.concatenate([high, low], axis=1)

    final = gathered(steps)
    back[at(steps), :] = final
    cot[...] = mm(final, dec_t[...])

    def backward(i, carry):
        k = steps - 1 - i
        c = cot[...]
        factor = twice(jnp.where(lenb[...] > k, stepb[...], 0.0))
        part = scaled[k]
        update = factor * (c + part)
        rounded = update.astype(BF16)
        value = acts[at(k), :].astype(F32)
        pre_grad = mm(rounded, w_out_t[...]) * (1.0 - value * value)
        pre_round = pre_grad.astype(BF16)
        seen = gathered(k)
        cot[...] = (
            c + factor * prior[...] * part + (mm(pre_round, w_in_t[...]) + mm(seen, dec_t[...]))
        )
        pre[at(k), :] = pre_round
        back[at(k), :] = seen
        upd_t[:, at(k)] = rounded.T
        sum_in[...] += jnp.sum(pre_grad.reshape(rows // 8, 8, hidden), axis=0)
        sum_out[...] += jnp.sum(update.reshape(rows // 8, 8, width), axis=0)
        return carry

    lax.fori_loop(0, steps, backward, 0, unroll=UNROLL)
    ginit[...] = cot[...]

    def weights(n, carry):
        cols = pl.ds(pl.multiple_of(n * width, width), width)
        grad_in = mm(traj_t[:, : steps * rows], pre[:, cols]) * scale
        grad_out = mm(upd_t[...], acts[:, cols]) * scale
        for h in range(2):
            big[h, :, n] = grad_in[:, h * rows : (h + 1) * rows].reshape(2, 4, 4, 8, rows)
            big[2 + h, :, n] = grad_out[:, h * rows : (h + 1) * rows].reshape(2, 4, 4, 8, rows)
        return carry

    lax.fori_loop(0, hidden // width, weights, 0)
    grad_dec = mm(traj_t[...], back[...]) * scale
    small[...] = jnp.zeros_like(small)
    small[:, :, :, 0] = (grad_dec[:, :rows] + grad_dec[:, rows:]).reshape(2, 4, 4, 8, rows)
    row_in = jnp.sum(sum_in[...], axis=0, keepdims=True) * scale
    row_out = jnp.sum(sum_out[...], axis=0, keepdims=True) * scale
    for r in range(hidden // rows):
        small[0, 0, 0, 1, r : r + 1, :] = row_in[:, r * rows : (r + 1) * rows]
    for r in range(width // rows):
        small[0, 0, 1, 1, r : r + 1, :] = row_out[:, r * rows : (r + 1) * rows]
    for r, part in ((2, loglik), (3, klacc[...])):
        whole = jnp.sum(jnp.sum(part, axis=0, keepdims=True), axis=1, keepdims=True) * scale
        small[0, 0, 1, 1, r : r + 1, :] = jnp.broadcast_to(whole, (1, rows))


def solve(total, init, brown, step, length, obs, observed, w_in, b_in, w_out, b_out, dec, prior, diff):
    steps, rows, width = brown.shape
    hidden, n_obs = w_in.shape[1], obs.shape[1]
    vmem = pltpu.VMEM
    return pl.pallas_call(
        functools.partial(solve_kernel, 1.0 / total),
        out_shape=(
            jax.ShapeDtypeStruct((1, rows), F32),
            jax.ShapeDtypeStruct((4, 2, 4, 4, 4, 8, rows), F32),
            jax.ShapeDtypeStruct((2, 4, 4, 2, 8, rows), F32),
            jax.ShapeDtypeStruct((rows, width), F32),
        ),
        in_specs=[pl.BlockSpec(memory_space=vmem)] * 13,
        out_specs=[pl.BlockSpec(memory_space=vmem)] * 4,
        scratch_shapes=[
            vmem((rows, width), F32),
            vmem((rows, rows), F32),
            vmem((rows, rows), jnp.int32),
            vmem((rows, width), F32),
            vmem((n_obs, rows, rows), jnp.int32),
            vmem((rows * n_obs, rows), F32),
            vmem((n_obs, rows, rows), F32),
            vmem((rows, rows), F32),
            vmem((width, (steps + 1) * rows), BF16),
            vmem((steps * rows, hidden), BF16),
            vmem((steps, rows, width), F32),
            vmem((steps * rows, hidden), BF16),
            vmem(((steps + 1) * rows, width), BF16),
            vmem((width, steps * rows), BF16),
            vmem((hidden, width), BF16),
            vmem((width, hidden), BF16),
            vmem((width, width), BF16),
            vmem((rows, width), F32),
            vmem((8, hidden), F32),
            vmem((8, width), F32),
        ],
        compiler_params=pltpu.CompilerParams(vmem_limit_bytes=58 * 1024 * 1024),
        name="solve",
    )(
        init, brown, step.reshape(1, -1), length.reshape(1, -1), obs, observed, w_in,
        b_in.reshape(1, -1), w_out, b_out.reshape(1, -1), dec, prior.reshape(1, -1), diff.reshape(1, -1),
    )


def on_device(
    init_state, brownian, step_size, lengths, obs_steps, observed,
    w_in, b_in, w_out, b_out, decoder, prior_rate, diffusion,
):
    total = init_state.shape[0] * lax.axis_size(BATCH_MP)
    share = w_in.shape[1]
    w_in_all = lax.all_gather(w_in, "mp", axis=1, tiled=True)
    w_out_all = lax.all_gather(w_out, "mp", axis=0, tiled=True)
    b_in_all = lax.all_gather(b_in, "mp", axis=0, tiled=True)
    elbo, big, small, grad_init = solve(
        total, init_state, brownian, step_size, lengths, obs_steps, observed,
        w_in_all, b_in_all, w_out_all, b_out, decoder, prior_rate, diffusion,
    )
    big, small = lax.psum((big, small), BATCH_MP)
    me = lax.axis_index("mp")
    own = lax.dynamic_index_in_dim(big, me, 2, keepdims=False)
    own = own.reshape(2, 2, 256, 128)
    own_in = jnp.concatenate([own[0, 0], own[0, 1]], axis=1)
    own_out = jnp.concatenate([own[1, 0], own[1, 1]], axis=1).T
    grad_dec = small[:, :, :, 0].reshape(256, 128)
    own_b = lax.dynamic_slice_in_dim(small[0, 0, 0, 1].reshape(-1), me * share, share, 0)
    tail = small[0, 0, 1, 1]
    return (
        elbo.reshape(-1), tail[2:4, 0], own_in, own_b, own_out, tail[0:2].reshape(-1), grad_dec, grad_init,
    )


def solution(mesh):
    torus = Mesh(
        mesh.devices.reshape(4, 4, 2, mesh.shape["mp"]), ("batch_0", "batch_1", "batch_2", "mp")
    )
    placed = (
        P(BATCH_MP, None), P(None, BATCH_MP, None), P(BATCH_MP), P(BATCH_MP), P(BATCH_MP, None),
        P(BATCH_MP, None, None), P(None, "mp"), P("mp"), P("mp", None), P(), P(), P(), P(),
    )
    return jax.shard_map(
        on_device,
        mesh=torus,
        in_specs=placed,
        out_specs=(
            P(BATCH_MP), P(), P(None, "mp"), P("mp"), P("mp", None), P(), P(), P(BATCH_MP, None),
        ),
        check_vma=False,
    )
```

time: 799 us -> 253 us (0.32); the launches traced: 789 us -> 253 us
  matrix products: 284 us -> 0 us
  local copies, waits for them, and re-layouts: 234 us -> 8.79 us
  waiting for transfers between devices: 70.5 us -> 160 us
  other arithmetic: 80.4 us -> 0.74 us
  blocking collectives: 100 us -> 31.6 us
  Pallas kernels: 0 us -> 37.7 us
    dot_general x196 -> x0, matrix products: 284 us -> none  [the longest x32 59.4 us: forward(): jnp.dot(current.astype(jnp.bfloat16), w_in_all, preferred_element_type=jn...]
    while x128 -> x0, local copies, waits for them, and re-layouts: 136 us -> none
    psum x1, waiting for transfers between devices: 50.8 us -> 160 us  [on_device(): big, small = lax.psum((big, small), BATCH_MP)]
    psum x5 -> x0, blocking collectives: 100 us -> none  [the longest x1 64.6 us: on_device(): lax.psum((sum_w_in, sum_b_in, sum_w_out, sum_b_out, decoder_grad), BATCH_MP)]
    dynamic_slice x64 -> x2, local copies, waits for them, and re-layouts: 71.6 us -> 1.72 us  [the longest x1 1.08 us: on_device(): own = lax.dynamic_index_in_dim(big, me, 2, keepdims=False)]
    reduce_sum x66 -> x0, other arithmetic: 66.1 us -> none  [the longest x32 32.5 us: forward(): jnp.sum(residual * residual, axis=1)]
    pallas_call x0 -> x1, Pallas kernels: none -> 37.7 us  [solve(): pl.pallas_call(functools.partial(solve_kernel, 1.0 / total), out_shape=(j...]
    all_gather x0 -> x3, blocking collectives: none -> 31.6 us  [the longest x1 13 us: on_device(): w_in_all = lax.all_gather(w_in, 'mp', axis=1, tiled=True)]
  transfers between devices with their start and end apart: 2 -> 1, of which waited for: 2 -> 1; matrix products, arithmetic and copies ran while one was open for 1% -> 0% of each run, Pallas kernels for 0% -> 0%
where the time goes in v1:
time: 253 us
  waiting for transfers between devices  160 us (63%)
  Pallas kernels  37.7 us (15%)
  blocking collectives  31.6 us (12%)
  between operations  14.1 us (6%)
  local copies, waits for them, and re-layouts  8.79 us (3%)
    psum x1, waiting for transfers between devices, on_device(): big, small = lax.psum((big, small), BATCH_MP)  160 us
    pallas_call x1, Pallas kernels, solve(): pl.pallas_call(functools.partial(solve_kernel, 1.0 / total), out_shape=(j...  37.7 us
    all_gather x1, blocking collectives, on_device(): w_in_all = lax.all_gather(w_in, 'mp', axis=1, tiled=True)  13 us
    all_gather x1, blocking collectives, on_device(): w_out_all = lax.all_gather(w_out, 'mp', axis=0, tiled=True)  11.9 us
    all_gather x1, blocking collectives, on_device(): b_in_all = lax.all_gather(b_in, 'mp', axis=0, tiled=True)  6.74 us
  transfers between devices with their start and end apart: 1, of which 1 were waited for; matrix products, arithmetic and copies ran while one was open for 0% of the time, Pallas kernels for 0%

profile of v1, /device:TPU:1, one launch (start us, length us, event | category | flops | bytes accessed | tf_op | source)
XLA Modules:
  0.0 253.1 jit_solution(8787977915554646952)
XLA Ops:
  7.2 0.0 all-reduce.3.cloned.1.call-start
  7.2 1.4 copy.25.obs
  8.6 13.0 %all_gather.9.w_in = bf16[256,1024]{1,0:T(8,128)(2,1)} all-gather(bf16[256,256]{1,0:T(8,128)(2,1)} %param.19), channel_id=1, replica_groups=mesh['batch_0'=4,'batch_1'=4,'batch_2'=2,'mp'=4] {'mp'}, dimensions={1}, use_global_device_ids=true | all-gather | bytes 655360 | tf_op jit(solution)/shard_map/all_gather | solution.py:205
  21.7 0.7 reshape.55
  22.3 6.7 %all-gather = bf16[4,1,256]{2,1,0:T(2,128)(2,1)} all-gather(bf16[1,1,256]{2,1,0:T(2,128)(2,1)S(1)} %reshape.55), channel_id=1, replica_groups=mesh['batch_0'=4,'batch_1'=4,'batch_2'=2,'mp'=4] {'mp'}, dimensions={0}, use_global_device_ids=true | all-gather | bytes 2560 | tf_op jit(solution)/shard_map/all_gather | solution.py:207
  29.1 11.9 %all_gather.11.w_out = bf16[1024,256]{1,0:T(8,128)(2,1)} all-gather(bf16[256,256]{1,0:T(8,128)(2,1)} %param.21), channel_id=1, replica_groups=mesh['batch_0'=4,'batch_1'=4,'batch_2'=2,'mp'=4] {'mp'}, dimensions={0}, use_global_device_ids=true | all-gather | bytes 655360 | tf_op jit(solution)/shard_map/all_gather | solution.py:206
  40.9 37.7 %solve.1 = (f32[1,128]{1,0:T(1,128)}, f32[4,2,4,4,4,8,128]{6,5,4,3,2,1,0:T(8,128)}, f32[2,4,4,2,8,128]{5,4,3,2,1,0:T(8,128)}, f32[128,256]{1,0:T(8,128)}) custom-call(f32[128,256]{1,0:T(8,128)} %init.1, bf16[32,128,256]{2,1,0:T(8,128)(2,1)} %brown.1, f32[1,128]{1,0:T(1,128)} %bitcast.31, s32[1,128]{1,0:T(1,128)} %bitcast.32, s32[128,8]{1,0:T(8,128)} %copy.25.obs, ...), custom_call_target="tpu_custom_call" | custom-call | tf_op jit(solution)/shard_map/solve/pallas_call | solution.py:159
  78.6 0.0 all-reduce.3.cloned.1.call-update
  78.6 160.2 %all-reduce.3.cloned.1.call-done = (f32[2,4,4,2,8,128]{5,4,3,2,1,0:T(8,128)}, f32[4,2,4,4,4,8,128]{6,5,4,3,2,1,0:T(8,128)}) async-done(((f32[2,4,4,2,8,128]{5,4,3,2,1,0:T(8,128)}, f32[4,2,4,4,4,8,128]{6,5,4,3,2,1,0:T(8,128)}), (f32[2,4,4,2,8,128]{5,4,3,2,1,0:T(8,128)}, f32[4,2,4,4,4,8,128]{6,5,4,3,2,1,0:T(8,128)})) %all-reduce.3.cloned.1.call-update) | async-done | bytes 2359312 | tf_op jit(solution)/shard_map/psum | solution.py:212
  238.8 0.7 slice_bitcast_fusion.4
  239.5 1.2 slice_bitcast_fusion.6
  240.7 1.6 slice.45
  242.3 0.6 slice_reduce_fusion
  242.9 1.1 constant_dynamic-slice_fusion
  244.1 0.7 pad_maximum_fusion
  244.8 0.8 copy.26
  245.6 0.6 dynamic_slice.8
  (1 shorter events, 0.0 us)
Async XLA Ops:
  7.2 231.6 %all-reduce.3.cloned.1.call-start = ((), (), s32[]{:S(2)}) async-start(), calls=%async_computation | async-start | bytes 4718592 | tf_op jit(solution)/shard_map/psum | solution.py:212
Sparse Core Ops, SparseCore 0:
  78.7 160.0 all-reduce.2

commit v2 on v1

--- a/solution.py
+++ b/solution.py
@@ -30,14 +30,13 @@
 ):
     steps, rows, width = brown.shape
     hidden = w_in.shape[1]
-    n_obs = obs.shape[1]
+    n_obs = obs.shape[0]
 
     stepb[...] = jnp.broadcast_to(step[...], (rows, rows)).T
     lenb[...] = jnp.broadcast_to(length[...], (rows, rows)).T
     dr[...] = diff[...] * twice(jnp.sqrt(stepb[...]))
-    obs_all = obs[...]
     for j in range(n_obs):
-        obsb[j] = jnp.broadcast_to(obs_all[:, j : j + 1], (rows, rows))
+        obsb[j] = jnp.broadcast_to(obs[j : j + 1, :], (rows, rows)).T
     obsf[...] = observed[...].astype(F32).reshape(rows * n_obs, dec.shape[1])
     w_in_t[...] = w_in[...].T
     w_out_t[...] = w_out[...].T
@@ -48,7 +47,7 @@
     sum_in[...] = jnp.zeros_like(sum_in)
     sum_out[...] = jnp.zeros_like(sum_out)
     state[...] = init[...]
-    bias = b_in[...].astype(F32)
+    bias = jnp.concatenate([b_in[m] for m in range(4)], axis=1).astype(F32)
     inv = 1.0 / diff[...]
 
     def see(k, rounded):
@@ -191,9 +190,270 @@
         compiler_params=pltpu.CompilerParams(vmem_limit_bytes=58 * 1024 * 1024),
         name="solve",
     )(
-        init, brown, step.reshape(1, -1), length.reshape(1, -1), obs, observed, w_in,
-        b_in.reshape(1, -1), w_out, b_out.reshape(1, -1), dec, prior.reshape(1, -1), diff.reshape(1, -1),
-    )
+        init, brown, step.reshape(1, -1), length.reshape(1, -1), obs.T, observed, w_in,
+        b_in, w_out, b_out.reshape(1, -1), dec, prior.reshape(1, -1), diff.reshape(1, -1),
+    )
+
+
+AXES = {"x": "mp", "y": "batch_0", "z": "batch_1", "c": "batch_2"}
+LOGICAL = pl.DeviceIdType.MESH
+ORDERS = ("xyz", "xyz", "yzx", "zxy")
+
+
+def far(axis, where):
+    return {AXES[axis]: where}
+
+
+def remote(src, dst, send, recv, to):
+    copy = pltpu.make_async_remote_copy(
+        src_ref=src, dst_ref=dst, send_sem=send, recv_sem=recv, device_id=to, device_id_type=LOGICAL
+    )
+    copy.start()
+    return copy
+
+
+def meet(peers):
+    barrier = pltpu.get_barrier_semaphore()
+    for peer in peers:
+        pl.semaphore_signal(barrier, inc=1, device_id=peer, device_id_type=LOGICAL)
+    pl.semaphore_wait(barrier, len(peers))
+
+
+def gather_kernel(w_in, w_out, b_in, wi, wo, bi, send, recv, bsend, brecv, psend, precv, local):
+    me, core = lax.axis_index("mp"), lax.axis_index("batch_2")
+    right, left, other = lax.rem(me + 1, 4), lax.rem(me + 3, 4), lax.rem(me + 2, 4)
+    depth, share = w_in.shape
+    half = depth // 2
+    upper = pl.ds(pl.multiple_of(core * half, half), half)
+    to_right, to_left, mate = far("x", right), far("x", left), far("c", 1 - core)
+    meet((to_right, to_left, far("x", other), mate))
+
+    def at_in(block):
+        return wi.at[upper, pl.ds(pl.multiple_of(block * share, share), share)]
+
+    def at_out(block):
+        return wo.at[pl.ds(pl.multiple_of(block * share + core * half, half), half), :]
+
+    own_in, own_out = w_in.at[upper, :], w_out.at[upper, :]
+    in_r = remote(own_in, at_in(me), send.at[0], recv.at[0], to_right)
+    out_l = remote(own_out, at_out(me), send.at[1], recv.at[1], to_left)
+    out_r = remote(own_out, at_out(me), send.at[2], recv.at[2], to_right)
+    in_l = remote(own_in, at_in(me), send.at[3], recv.at[3], to_left)
+    biases = [
+        remote(b_in, bi.at[me], bsend.at[d], brecv.at[d], far("x", lax.rem(me + d, 4)))
+        for d in (1, 2, 3)
+    ]
+    kept = [
+        pltpu.make_async_copy(w_in, wi.at[:, pl.ds(pl.multiple_of(me * share, share), share)], local.at[0]),
+        pltpu.make_async_copy(w_out, wo.at[pl.ds(pl.multiple_of(me * share, share), share), :], local.at[1]),
+        pltpu.make_async_copy(b_in, bi.at[me], local.at[2]),
+    ]
+    for copy in kept:
+        copy.start()
+    sent = []
+
+    def share_with_mate(n, ref):
+        sent.append(remote(ref, ref, psend.at[n], precv.at[n], mate))
+
+    in_r.wait_recv()
+    in_rr = remote(at_in(left), at_in(left), send.at[4], recv.at[4], to_right)
+    share_with_mate(0, at_in(left))
+    out_l.wait_recv()
+    out_ll = remote(at_out(right), at_out(right), send.at[5], recv.at[5], to_left)
+    share_with_mate(1, at_out(right))
+    out_r.wait_recv()
+    share_with_mate(2, at_out(left))
+    in_l.wait_recv()
+    share_with_mate(3, at_in(right))
+    in_rr.wait_recv()
+    share_with_mate(4, at_in(other))
+    out_ll.wait_recv()
+    share_with_mate(5, at_out(other))
+    for copy in kept:
+        copy.wait()
+    for copy in biases + sent:
+        copy.wait()
+    for copy in (in_r, out_l, out_r, in_l, in_rr, out_ll):
+        copy.wait_send()
+
+
+def gather(w_in, w_out, b_in):
+    depth, share = w_in.shape
+    vmem, dma = pltpu.VMEM, pltpu.SemaphoreType.DMA
+    return pl.pallas_call(
+        gather_kernel,
+        out_shape=(
+            jax.ShapeDtypeStruct((depth, 4 * share), BF16),
+            jax.ShapeDtypeStruct((4 * share, depth), BF16),
+            jax.ShapeDtypeStruct((4, 1, share), BF16),
+        ),
+        in_specs=[pl.BlockSpec(memory_space=vmem)] * 3,
+        out_specs=[pl.BlockSpec(memory_space=vmem)] * 3,
+        scratch_shapes=[dma((6,)), dma((6,)), dma((4,)), dma((4,)), dma((6,)), dma((6,)), dma((3,))],
+        compiler_params=pltpu.CompilerParams(collective_id=0, has_side_effects=True),
+        name="gather",
+    )(w_in, w_out, b_in.reshape(1, -1))
+
+
+def reduce_kernel(
+    big, small, out,
+    got, cur, small_got, small_cur, r1, r2, r3, s1, s2, sx, fin,
+    dsend, drecv, send, recv, gsend, grecv, hsend, hrecv,
+):
+    place = {a: lax.axis_index(AXES[a]) for a in "xyzc"}
+    core = place["c"]
+    mate = far("c", 1 - core)
+
+    def other(axis, d):
+        return lax.rem(place[axis] + d, 4)
+
+    plane = [(dy, dz) for dy in range(4) for dz in range(4) if (dy, dz) != (0, 0)]
+
+    def in_plane(dy, dz):
+        return {AXES["y"]: other("y", dy), AXES["z"]: other("z", dz)}
+
+    peers = [mate] + [far("x", other("x", d)) for d in (1, 2, 3)] + [in_plane(*p) for p in plane]
+    meet(peers)
+
+    pending = []
+    first = [remote(big.at[u, 1 - core], got.at[u], dsend.at[u], drecv.at[u], mate) for u in range(4)]
+    first.append(remote(small.at[1 - core], small_got, dsend.at[4], drecv.at[4], mate))
+    pending += first
+
+    boxes = (r1, r2, r3)
+
+    def pick(ref, dims, axis, index):
+        return ref.at[tuple(index if a == axis else slice(None) for a in dims)]
+
+    def start(flow, stage, ref, dims, axis, box):
+        copies = []
+        for d in (1, 2, 3):
+            n = (flow * 3 + stage) * 3 + d - 1
+            copies.append(
+                remote(
+                    pick(ref, dims, axis, other(axis, d)), box.at[d - 1], send.at[n], recv.at[n],
+                    far(axis, other(axis, d)),
+                )
+            )
+        pending.extend(copies)
+        return copies
+
+    def finish(copies, ref, dims, axis, box):
+        for copy in copies:
+            copy.wait_recv()
+        mine = pick(ref, dims, axis, place[axis])[...]
+        return mine + box[0] + box[1] + box[2]
+
+    flying = {}
+    for u in (2, 3, 0, 1):
+        first[u].wait_recv()
+        cur[u] = big[u, core] + got[u]
+        flying[u] = start(u, 0, cur.at[u], "xyz", ORDERS[u][0], r1.at[u])
+    first[4].wait_recv()
+    small_cur[...] = small[core] + small_got[...]
+    flying[4] = start(4, 0, small_cur, "yz", "y", s1)
+
+    s = finish(flying[4], small_cur, "yz", "y", s1)
+    small_got[0] = s
+    flying[4] = start(4, 1, small_got.at[0], "z", "z", s2)
+    for u in (2, 3, 0, 1):
+        axis = ORDERS[u][0]
+        got[u, 0] = finish(flying[u], cur.at[u], "xyz", axis, r1.at[u])
+        dims = "xyz".replace(axis, "")
+        flying[u] = start(u, 1, got.at[u, 0], dims, ORDERS[u][1], r2.at[u])
+    s = finish(flying[4], small_got.at[0], "z", "z", s2)
+    small_got[1, 0] = s
+    xs = []
+    for d in (1, 2, 3):
+        n = (4 * 3 + 2) * 3 + d - 1
+        xs.append(remote(small_got.at[1, 0], sx.at[place["x"]], send.at[n], recv.at[n], far("x", other("x", d))))
+    pending.extend(xs)
+    sx[place["x"]] = s
+    for u in (2, 3, 0, 1):
+        axis = ORDERS[u][1]
+        dims = "xyz".replace(ORDERS[u][0], "")
+        got[u, 1, 0] = finish(flying[u], got.at[u, 0], dims, axis, r2.at[u])
+        flying[u] = start(u, 2, got.at[u, 1, 0], ORDERS[u][2], ORDERS[u][2], r3.at[u])
+    for copy in xs:
+        copy.wait_recv()
+    fin[4:6] = sx[0] + sx[1] + sx[2] + sx[3]
+    for u in (2, 3, 0, 1):
+        fin[u] = finish(flying[u], got.at[u, 1, 0], ORDERS[u][2], ORDERS[u][2], r3.at[u])
+
+    home = out.at[core, place["y"], place["z"]]
+    spread = []
+    for n, (dy, dz) in enumerate(plane):
+        spread.append(remote(fin, home, gsend.at[n], grecv.at[n], in_plane(dy, dz)))
+    pair = [remote(fin, home, hsend.at[15], hrecv.at[15], mate)]
+    out[core, place["y"], place["z"]] = fin[...]
+    for n, (dy, dz) in enumerate(plane):
+        spread[n].wait_recv()
+        came = out.at[core, lax.rem(place["y"] + 4 - dy, 4), lax.rem(place["z"] + 4 - dz, 4)]
+        pair.append(remote(came, came, hsend.at[n], hrecv.at[n], mate))
+    for copy in pair:
+        copy.wait()
+    for copy in pending + spread:
+        copy.wait_send()
+
+
+def reduce(big, small):
+    vmem, dma = pltpu.VMEM, pltpu.SemaphoreType.DMA
+    tile = (8, 128)
+    return pl.pallas_call(
+        reduce_kernel,
+        out_shape=jax.ShapeDtypeStruct((2, 4, 4, 6) + tile, F32),
+        in_specs=[pl.BlockSpec(memory_space=vmem)] * 2,
+        out_specs=pl.BlockSpec(memory_space=vmem),
+        scratch_shapes=[
+            vmem((4, 4, 4, 4) + tile, F32),
+            vmem((4, 4, 4, 4) + tile, F32),
+            vmem((4, 4, 2) + tile, F32),
+            vmem((4, 4, 2) + tile, F32),
+            vmem((4, 3, 4, 4) + tile, F32),
+            vmem((4, 3, 4) + tile, F32),
+            vmem((4, 3) + tile, F32),
+            vmem((3, 4, 2) + tile, F32),
+            vmem((3, 2) + tile, F32),
+            vmem((4, 2) + tile, F32),
+            vmem((6,) + tile, F32),
+            dma((5,)), dma((5,)), dma((45,)), dma((45,)), dma((15,)), dma((15,)), dma((16,)), dma((16,)),
+        ],
+        compiler_params=pltpu.CompilerParams(
+            collective_id=1, has_side_effects=True, vmem_limit_bytes=24 * 1024 * 1024
+        ),
+        name="reduce",
+    )(big, small)
+
+
+def finish_kernel(out, w_in, w_out, dec, b_in, b_out, scores):
+    me = lax.axis_index("mp")
+
+    def whole(u):
+        return out[:, :, :, u].reshape(256, 128)
+
+    w_in[:, :128] = whole(0)
+    w_in[:, 128:] = whole(1)
+    w_out[:128, :] = whole(2).T
+    w_out[128:, :] = whole(3).T
+    dec[...] = whole(4)
+    for r in range(2):
+        b_in[:, r * 128 : (r + 1) * 128] = out[0, 0, 0, 5, pl.ds(2 * me + r, 1), :]
+        b_out[:, r * 128 : (r + 1) * 128] = out[0, 0, 1, 5, r : r + 1, :]
+    scores[...] = out[0, 0, 1, 5, 2:4, :]
+
+
+def unpack(out):
+    vmem = pltpu.VMEM
+    return pl.pallas_call(
+        finish_kernel,
+        out_shape=tuple(
+            jax.ShapeDtypeStruct(s, F32)
+            for s in ((256, 256), (256, 256), (256, 128), (1, 256), (1, 256), (2, 128))
+        ),
+        in_specs=[pl.BlockSpec(memory_space=vmem)],
+        out_specs=[pl.BlockSpec(memory_space=vmem)] * 6,
+        name="unpack",
+    )(out)
 
 
 def on_device(
@@ -201,25 +461,15 @@
     w_in, b_in, w_out, b_out, decoder, prior_rate, diffusion,
 ):
     total = init_state.shape[0] * lax.axis_size(BATCH_MP)
-    share = w_in.shape[1]
-    w_in_all = lax.all_gather(w_in, "mp", axis=1, tiled=True)
-    w_out_all = lax.all_gather(w_out, "mp", axis=0, tiled=True)
-    b_in_all = lax.all_gather(b_in, "mp", axis=0, tiled=True)
+    w_in_all, w_out_all, b_in_all = gather(w_in, w_out, b_in)
     elbo, big, small, grad_init = solve(
         total, init_state, brownian, step_size, lengths, obs_steps, observed,
         w_in_all, b_in_all, w_out_all, b_out, decoder, prior_rate, diffusion,
     )
-    big, small = lax.psum((big, small), BATCH_MP)
-    me = lax.axis_index("mp")
-    own = lax.dynamic_index_in_dim(big, me, 2, keepdims=False)
-    own = own.reshape(2, 2, 256, 128)
-    own_in = jnp.concatenate([own[0, 0], own[0, 1]], axis=1)
-    own_out = jnp.concatenate([own[1, 0], own[1, 1]], axis=1).T
-    grad_dec = small[:, :, :, 0].reshape(256, 128)
-    own_b = lax.dynamic_slice_in_dim(small[0, 0, 0, 1].reshape(-1), me * share, share, 0)
-    tail = small[0, 0, 1, 1]
+    own_in, own_out, grad_dec, own_b, grad_b_out, scores = unpack(reduce(big, small))
     return (
-        elbo.reshape(-1), tail[2:4, 0], own_in, own_b, own_out, tail[0:2].reshape(-1), grad_dec, grad_init,
+        elbo.reshape(-1), scores[:, 0], own_in, own_b.reshape(-1), own_out, grad_b_out.reshape(-1),
+        grad_dec, grad_init,
     )
 
 

time: 253 us -> 95.5 us (0.38)
  waiting for transfers between devices: 160 us -> 0 us
  Pallas kernels: 37.7 us -> 88.7 us
  blocking collectives: 31.6 us -> 0 us
  between operations: 14.1 us -> 0.66 us
  local copies, waits for them, and re-layouts: 8.79 us -> 5.91 us
    psum x1 -> x0, waiting for transfers between devices: 160 us -> none  [on_device(): big, small = lax.psum((big, small), BATCH_MP)]
    pallas_call x0 -> x3, Pallas kernels: none -> 51 us  [the longest x1 34.7 us: reduce(): pl.pallas_call(reduce_kernel, out_shape=jax.ShapeDtypeStruct((2, 4, 4, 6)...]
    all_gather x3 -> x0, blocking collectives: 31.6 us -> none  [the longest x1 13 us: on_device(): w_in_all = lax.all_gather(w_in, 'mp', axis=1, tiled=True)]
  transfers between devices with their start and end apart: 1 -> 0, of which waited for: 1 -> 0; matrix products, arithmetic and copies ran while one was open for 0% -> 0% of each run, Pallas kernels for 0% -> 0%
where the time goes in v2:
time: 95.5 us; the launch traced here: 95.3 us
  Pallas kernels  88.7 us (93%)
  local copies, waits for them, and re-layouts  5.91 us (6%)
    pallas_call x1, Pallas kernels, solve(): pl.pallas_call(functools.partial(solve_kernel, 1.0 / total), out_shape=(j...  37.7 us
    pallas_call x1, Pallas kernels, reduce(): pl.pallas_call(reduce_kernel, out_shape=jax.ShapeDtypeStruct((2, 4, 4, 6)...  34.7 us
    pallas_call x1, Pallas kernels, gather(): pl.pallas_call(gather_kernel, out_shape=(jax.ShapeDtypeStruct((depth, 4 *...  14.4 us
    unnamed x6, local copies, waits for them, and re-layouts  3.42 us
    pallas_call x1, Pallas kernels, unpack(): pl.pallas_call(finish_kernel, out_shape=tuple((jax.ShapeDtypeStruct(s, F3...  2.04 us

profile of v2, /device:TPU:1, one launch (start us, length us, event | category | flops | bytes accessed | tf_op | source)
XLA Modules:
  0.0 95.3 jit_solution(1505534074361118470)
XLA Ops:
  0.6 1.2 %reshape.45.b_in = bf16[1,256]{1,0:T(2,128)(2,1)} reshape(bf16[256]{0:T(256)(128)(2,1)} %param.20) | data formatting | bytes 1024 | tf_op jit(solution)/shard_map/reshape | solution.py:295
  1.9 14.4 %gather.1 = (bf16[256,1024]{1,0:T(8,128)(2,1)}, bf16[1024,256]{1,0:T(8,128)(2,1)}, bf16[4,1,256]{2,1,0:T(2,128)(2,1)}) custom-call(bf16[256,256]{1,0:T(8,128)(2,1)} %w_in.1, bf16[256,256]{1,0:T(8,128)(2,1)} %w_out.1, bf16[1,256]{1,0:T(2,128)(2,1)} %reshape.45.b_in), custom_call_target="tpu_custom_call" | custom-call | tf_op jit(solution)/shard_map/gather/pallas_call | solution.py:283
  16.2 37.7 %solve.1 = (f32[1,128]{1,0:T(1,128)}, f32[4,2,4,4,4,8,128]{6,5,4,3,2,1,0:T(8,128)}, f32[2,4,4,2,8,128]{5,4,3,2,1,0:T(8,128)}, f32[128,256]{1,0:T(8,128)}) custom-call(f32[128,256]{1,0:T(8,128)} %init.1, bf16[32,128,256]{2,1,0:T(8,128)(2,1)} %brown.1, f32[1,128]{1,0:T(1,128)} %bitcast.13, s32[1,128]{1,0:T(1,128)} %bitcast.14, s32[8,128]{1,0:T(8,128)} %bitcast.9, ...), custom_call_target="tpu_custom_call" | custom-call | tf_op jit(solution)/shard_map/solve/pallas_call | solution.py:158
  53.9 0.0 copy-start.1
  53.9 1.6 %copy-done.1 = f32[4,2,4,4,4,8,128]{6,5,4,3,2,1,0:T(8,128)S(1)} copy-done((f32[4,2,4,4,4,8,128]{6,5,4,3,2,1,0:T(8,128)S(1)}, f32[4,2,4,4,4,8,128]{6,5,4,3,2,1,0:T(8,128)}, u32[]{:S(2)}) %copy-start.1) | copy-done | bytes 2097176
  55.5 0.0 copy-start.2
  55.5 0.9 copy-done.2
  56.4 34.7 %reduce.3.out = f32[2,4,4,6,8,128]{5,4,3,2,1,0:T(8,128)S(1)} custom-call(f32[4,2,4,4,4,8,128]{6,5,4,3,2,1,0:T(8,128)S(1)} %copy-done.1, f32[2,4,4,2,8,128]{5,4,3,2,1,0:T(8,128)S(1)} %copy-done.2), custom_call_target="tpu_custom_call" | custom-call | tf_op jit(solution)/shard_map/reduce/pallas_call | solution.py:402
  91.1 0.0 copy-start
  91.1 0.9 copy-done
  92.0 2.0 %unpack.1 = (f32[256,256]{1,0:T(8,128)}, f32[256,256]{1,0:T(8,128)}, f32[256,128]{1,0:T(8,128)}, f32[1,256]{1,0:T(1,128)}, f32[1,256]{1,0:T(1,128)}, /*index=5*/f32[2,128]{1,0:T(2,128)}) custom-call(f32[2,4,4,6,8,128]{5,4,3,2,1,0:T(8,128)} %copy-done), custom_call_target="tpu_custom_call" | custom-call | tf_op jit(solution)/shard_map/unpack/pallas_call | solution.py:447
  94.0 1.3 %slice_reduce_fusion = f32[2]{0:T(128)} fusion(f32[2,128]{1,0:T(2,128)} %get-tuple-element.27), kind=kLoop, calls=%fused_computation | loop fusion | bytes 16 | tf_op jit(solution)/shard_map/slice | solution.py:471
Async XLA Ops:
  53.9 1.6 %copy-start.1 = (f32[4,2,4,4,4,8,128]{6,5,4,3,2,1,0:T(8,128)S(1)}, f32[4,2,4,4,4,8,128]{6,5,4,3,2,1,0:T(8,128)}, u32[]{:S(2)}) copy-start(f32[4,2,4,4,4,8,128]{6,5,4,3,2,1,0:T(8,128)} %get-tuple-element.25.big) | copy-start | bytes 6291460
  55.5 0.9 copy-start.2
  91.1 0.9 copy-start

commit v3 on v1

--- a/solution.py
+++ b/solution.py
@@ -21,35 +21,140 @@
     return jnp.concatenate([a, a], axis=1)
 
 
-def solve_kernel(
+AXES = {"x": "mp", "y": "batch_0", "z": "batch_1", "c": "batch_2"}
+LOGICAL = pl.DeviceIdType.MESH
+ORDERS = ("xyz", "xyz", "yzx", "zxy")
+
+
+def far(axis, where):
+    return {AXES[axis]: where}
+
+
+def remote(src, dst, send, recv, to):
+    copy = pltpu.make_async_remote_copy(
+        src_ref=src, dst_ref=dst, send_sem=send, recv_sem=recv, device_id=to, device_id_type=LOGICAL
+    )
+    copy.start()
+    return copy
+
+
+def meet(peers):
+    barrier = pltpu.get_barrier_semaphore()
+    for peer in peers:
+        pl.semaphore_signal(barrier, inc=1, device_id=peer, device_id_type=LOGICAL)
+    pl.semaphore_wait(barrier, len(peers))
+
+
+def whole_kernel(
     scale,
-    init, brown, step, length, obs, observed, w_in, b_in, w_out, b_out, dec, prior, diff,
-    elbo, big, small, ginit,
+    init, brown_hbm, step, length, obs, observed_hbm, w_in, b_in, w_out, b_out, dec, prior, diff,
+    elbo, out, ginit,
+    wi, wo, bi, brown, observed,
     state, stepb, lenb, dr, obsb, obsf, acc, klacc, traj_t, acts, scaled, pre, back, upd_t,
     w_in_t, w_out_t, dec_t, cot, sum_in, sum_out,
+    big, small, got, cur, small_got, small_cur, r1, r2, r3, s1, s2, sx, fin,
+    wsend, wrecv, bsend, brecv, psend, precv, local,
+    dsend, drecv, send, recv, gsend, grecv, hsend, hrecv,
 ):
     steps, rows, width = brown.shape
-    hidden = w_in.shape[1]
-    n_obs = obs.shape[1]
+    hidden = wi.shape[1]
+    n_obs = obs.shape[0]
+    loads = [
+        pltpu.make_async_copy(observed_hbm, observed, local.at[3]),
+        pltpu.make_async_copy(brown_hbm, brown, local.at[4]),
+    ]
+    for copy in loads:
+        copy.start()
+
+    place = {a: lax.axis_index(AXES[a]) for a in "xyzc"}
+    me, core = place["x"], place["c"]
+    mate = far("c", 1 - core)
+
+    def other(axis, d):
+        return lax.rem(place[axis] + d, 4)
+
+    plane = [(dy, dz) for dy in range(4) for dz in range(4) if (dy, dz) != (0, 0)]
+
+    def in_plane(dy, dz):
+        return {AXES["y"]: other("y", dy), AXES["z"]: other("z", dz)}
+
+    meet([mate] + [far("x", other("x", d)) for d in (1, 2, 3)] + [in_plane(*p) for p in plane])
+
+    right, left, across = other("x", 1), other("x", 3), other("x", 2)
+    depth, share = w_in.shape
+    half = depth // 2
+    upper = pl.ds(pl.multiple_of(core * half, half), half)
+    to_right, to_left = far("x", right), far("x", left)
+
+    def at_in(block):
+        return wi.at[upper, pl.ds(pl.multiple_of(block * share, share), share)]
+
+    def at_out(block):
+        return wo.at[pl.ds(pl.multiple_of(block * share + core * half, half), half), :]
+
+    own_in, own_out = w_in.at[upper, :], w_out.at[upper, :]
+    in_r = remote(own_in, at_in(me), wsend.at[0], wrecv.at[0], to_right)
+    out_l = remote(own_out, at_out(me), wsend.at[1], wrecv.at[1], to_left)
+    out_r = remote(own_out, at_out(me), wsend.at[2], wrecv.at[2], to_right)
+    in_l = remote(own_in, at_in(me), wsend.at[3], wrecv.at[3], to_left)
+    biases = [
+        remote(b_in, bi.at[me], bsend.at[d], brecv.at[d], far("x", other("x", d))) for d in (1, 2, 3)
+    ]
+    kept = [
+        pltpu.make_async_copy(w_in, wi.at[:, pl.ds(pl.multiple_of(me * share, share), share)], local.at[0]),
+        pltpu.make_async_copy(w_out, wo.at[pl.ds(pl.multiple_of(me * share, share), share), :], local.at[1]),
+        pltpu.make_async_copy(b_in, bi.at[me], local.at[2]),
+    ]
+    for copy in kept:
+        copy.start()
 
     stepb[...] = jnp.broadcast_to(step[...], (rows, rows)).T
     lenb[...] = jnp.broadcast_to(length[...], (rows, rows)).T
     dr[...] = diff[...] * twice(jnp.sqrt(stepb[...]))
-    obs_all = obs[...]
     for j in range(n_obs):
-        obsb[j] = jnp.broadcast_to(obs_all[:, j : j + 1], (rows, rows))
-    obsf[...] = observed[...].astype(F32).reshape(rows * n_obs, dec.shape[1])
-    w_in_t[...] = w_in[...].T
-    w_out_t[...] = w_out[...].T
+        obsb[j] = jnp.broadcast_to(obs[j : j + 1, :], (rows, rows)).T
     dec_flip = dec[...].T
     dec_t[...] = jnp.concatenate([dec_flip, dec_flip], axis=0)
     klacc[...] = jnp.zeros_like(klacc)
     acc[...] = jnp.zeros_like(acc)
     sum_in[...] = jnp.zeros_like(sum_in)
     sum_out[...] = jnp.zeros_like(sum_out)
+    small[...] = jnp.zeros_like(small)
     state[...] = init[...]
-    bias = b_in[...].astype(F32)
     inv = 1.0 / diff[...]
+    loads[0].wait()
+    obsf[...] = observed[...].astype(F32).reshape(rows * n_obs, dec.shape[1])
+
+    sent = []
+
+    def share_with_mate(n, ref):
+        sent.append(remote(ref, ref, psend.at[n], precv.at[n], mate))
+
+    in_r.wait_recv()
+    in_rr = remote(at_in(left), at_in(left), wsend.at[4], wrecv.at[4], to_right)
+    share_with_mate(0, at_in(left))
+    out_l.wait_recv()
+    out_ll = remote(at_out(right), at_out(right), wsend.at[5], wrecv.at[5], to_left)
+    share_with_mate(1, at_out(right))
+    out_r.wait_recv()
+    share_with_mate(2, at_out(left))
+    in_l.wait_recv()
+    share_with_mate(3, at_in(right))
+    in_rr.wait_recv()
+    share_with_mate(4, at_in(across))
+    out_ll.wait_recv()
+    share_with_mate(5, at_out(across))
+    for copy in kept:
+        copy.wait()
+    for copy in biases + sent:
+        copy.wait()
+    for copy in (in_r, out_l, out_r, in_l, in_rr, out_ll):
+        copy.wait_send()
+
+    w_in_t[...] = wi[...].T
+    w_out_t[...] = wo[...].T
+    bias = jnp.concatenate([bi[m] for m in range(4)], axis=1).astype(F32)
+    loads[1].wait()
 
     def see(k, rounded):
         seen = mm(rounded, dec[...])
@@ -62,14 +167,17 @@
     def forward(k, carry):
         s = state[...]
         rounded = s.astype(BF16)
-        activity = jnp.tanh(mm(rounded, w_in[...]) + bias).astype(BF16)
-        drift = mm(activity, w_out[...]) + b_out[...]
+        drift = b_out[...]
+        for n in range(0, hidden, width):
+            cs = slice(n, n + width)
+            activity = jnp.tanh(mm(rounded, wi[:, cs]) + bias[:, cs]).astype(BF16)
+            acts[at(k), cs] = activity
+            drift = drift + mm(activity, wo[cs, :])
         live = lenb[...] > k
         factor = jnp.where(live, stepb[...], 0.0)
         residual = (drift + prior[...] * s) * inv
         noise = dr[...] * brown[k].astype(F32)
         state[...] = s + twice(factor) * drift + jnp.where(twice(live), noise, 0.0)
-        acts[at(k), :] = activity
         scaled[k] = residual * inv
         square = residual * residual
         klacc[...] += (0.5 * factor) * (square[:, :rows] + square[:, rows:])
@@ -128,18 +236,49 @@
     lax.fori_loop(0, steps, backward, 0, unroll=UNROLL)
     ginit[...] = cot[...]
 
-    def weights(n, carry):
+    pending = []
+    first = {}
+    flying = {}
+
+    def pick(ref, dims, axis, index):
+        return ref.at[tuple(index if a == axis else slice(None) for a in dims)]
+
+    def hop(flow, stage, d, src, box, axis):
+        n = (flow * 3 + stage) * 3 + d - 1
+        copy = remote(src, box.at[d - 1], send.at[n], recv.at[n], far(axis, other(axis, d)))
+        pending.append(copy)
+        flying.setdefault((flow, stage), []).append(copy)
+
+    def start(flow, stage, ref, dims, axis, box):
+        for d in (2, 1, 3):
+            hop(flow, stage, d, pick(ref, dims, axis, other(axis, d)), box, axis)
+
+    def finish(flow, stage, ref, dims, axis, box):
+        for copy in flying[flow, stage]:
+            copy.wait_recv()
+        mine = pick(ref, dims, axis, place[axis])[...]
+        return mine + box[0] + box[1] + box[2]
+
+    def to_mate(n, src, dst):
+        copy = remote(src, dst, dsend.at[n], drecv.at[n], mate)
+        pending.append(copy)
+        return copy
+
+    def grads(d, base, left_ref, right_ref):
+        n = other("x", d)
         cols = pl.ds(pl.multiple_of(n * width, width), width)
-        grad_in = mm(traj_t[:, : steps * rows], pre[:, cols]) * scale
-        grad_out = mm(upd_t[...], acts[:, cols]) * scale
+        grad = mm(left_ref[:, : steps * rows], right_ref[:, cols]) * scale
         for h in range(2):
-            big[h, :, n] = grad_in[:, h * rows : (h + 1) * rows].reshape(2, 4, 4, 8, rows)
-            big[2 + h, :, n] = grad_out[:, h * rows : (h + 1) * rows].reshape(2, 4, 4, 8, rows)
-        return carry
-
-    lax.fori_loop(0, hidden // width, weights, 0)
+            u = base + h
+            big[u, :, n] = grad[:, h * rows : (h + 1) * rows].reshape(2, 4, 4, 8, rows)
+        for h in range(2):
+            u = base + h
+            first[u, d] = to_mate(u * 4 + d, big.at[u, 1 - core, n], got.at[u, n])
+
+    for d in (2, 1, 3, 0):
+        grads(d, 0, traj_t, pre)
+
     grad_dec = mm(traj_t[...], back[...]) * scale
-    small[...] = jnp.zeros_like(small)
     small[:, :, :, 0] = (grad_dec[:, :rows] + grad_dec[:, rows:]).reshape(2, 4, 4, 8, rows)
     row_in = jnp.sum(sum_in[...], axis=0, keepdims=True) * scale
     row_out = jnp.sum(sum_out[...], axis=0, keepdims=True) * scale
@@ -148,25 +287,90 @@
     for r in range(width // rows):
         small[0, 0, 1, 1, r : r + 1, :] = row_out[:, r * rows : (r + 1) * rows]
     for r, part in ((2, loglik), (3, klacc[...])):
-        whole = jnp.sum(jnp.sum(part, axis=0, keepdims=True), axis=1, keepdims=True) * scale
-        small[0, 0, 1, 1, r : r + 1, :] = jnp.broadcast_to(whole, (1, rows))
-
-
-def solve(total, init, brown, step, length, obs, observed, w_in, b_in, w_out, b_out, dec, prior, diff):
+        total = jnp.sum(jnp.sum(part, axis=0, keepdims=True), axis=1, keepdims=True) * scale
+        small[0, 0, 1, 1, r : r + 1, :] = jnp.broadcast_to(total, (1, rows))
+    first[4] = to_mate(16, small.at[1 - core], small_got)
+
+    for d in (2, 1, 3, 0):
+        grads(d, 2, upd_t, acts)
+        n = other("x", d)
+        for u in (0, 1):
+            first[u, d].wait_recv()
+            cur[u, n] = big[u, core, n] + got[u, n]
+            if d:
+                hop(u, 0, d, cur.at[u, n], r1.at[u], "x")
+    first[4].wait_recv()
+    small_cur[...] = small[core] + small_got[...]
+    start(4, 0, small_cur, "yz", "y", s1)
+    for u in (2, 3):
+        for d in (2, 1, 3, 0):
+            first[u, d].wait_recv()
+        cur[u] = big[u, core] + got[u]
+        start(u, 0, cur.at[u], "xyz", ORDERS[u][0], r1.at[u])
+
+    small_got[0] = finish(4, 0, small_cur, "yz", "y", s1)
+    start(4, 1, small_got.at[0], "z", "z", s2)
+    for u in (0, 1, 2, 3):
+        axis = ORDERS[u][0]
+        got[u, 0] = finish(u, 0, cur.at[u], "xyz", axis, r1.at[u])
+        dims = "xyz".replace(axis, "")
+        start(u, 1, got.at[u, 0], dims, ORDERS[u][1], r2.at[u])
+    s = finish(4, 1, small_got.at[0], "z", "z", s2)
+    small_got[1, 0] = s
+    for d in (1, 2, 3):
+        n = (4 * 3 + 2) * 3 + d - 1
+        copy = remote(small_got.at[1, 0], sx.at[me], send.at[n], recv.at[n], far("x", other("x", d)))
+        pending.append(copy)
+        flying.setdefault((4, 2), []).append(copy)
+    sx[me] = s
+    for u in (0, 1, 2, 3):
+        axis = ORDERS[u][1]
+        dims = "xyz".replace(ORDERS[u][0], "")
+        got[u, 1, 0] = finish(u, 1, got.at[u, 0], dims, axis, r2.at[u])
+        start(u, 2, got.at[u, 1, 0], ORDERS[u][2], ORDERS[u][2], r3.at[u])
+    for copy in flying[4, 2]:
+        copy.wait_recv()
+    fin[4:6] = sx[0] + sx[1] + sx[2] + sx[3]
+    for u in (0, 1, 2, 3):
+        fin[u] = finish(u, 2, got.at[u, 1, 0], ORDERS[u][2], ORDERS[u][2], r3.at[u])
+
+    home = out.at[core, place["y"], place["z"]]
+    spread = []
+    for n, (dy, dz) in enumerate(plane):
+        spread.append(remote(fin, home, gsend.at[n], grecv.at[n], in_plane(dy, dz)))
+    pair = [remote(fin, home, hsend.at[15], hrecv.at[15], mate)]
+    out[core, place["y"], place["z"]] = fin[...]
+    for n, (dy, dz) in enumerate(plane):
+        spread[n].wait_recv()
+        came = out.at[core, lax.rem(place["y"] + 4 - dy, 4), lax.rem(place["z"] + 4 - dz, 4)]
+        pair.append(remote(came, came, hsend.at[n], hrecv.at[n], mate))
+    for copy in pair:
+        copy.wait()
+    for copy in pending + spread:
+        copy.wait_send()
+
+
+def whole(total, init, brown, step, length, obs, observed, w_in, b_in, w_out, b_out, dec, prior, diff):
     steps, rows, width = brown.shape
-    hidden, n_obs = w_in.shape[1], obs.shape[1]
-    vmem = pltpu.VMEM
+    hidden, n_obs = 4 * w_in.shape[1], obs.shape[1]
+    vmem, dma = pltpu.VMEM, pltpu.SemaphoreType.DMA
+    near, rest = pl.BlockSpec(memory_space=vmem), pl.BlockSpec(memory_space=pl.ANY)
+    tile = (8, 128)
     return pl.pallas_call(
-        functools.partial(solve_kernel, 1.0 / total),
+        functools.partial(whole_kernel, 1.0 / total),
         out_shape=(
             jax.ShapeDtypeStruct((1, rows), F32),
-            jax.ShapeDtypeStruct((4, 2, 4, 4, 4, 8, rows), F32),
-            jax.ShapeDtypeStruct((2, 4, 4, 2, 8, rows), F32),
+            jax.ShapeDtypeStruct((2, 4, 4, 6) + tile, F32),
             jax.ShapeDtypeStruct((rows, width), F32),
         ),
-        in_specs=[pl.BlockSpec(memory_space=vmem)] * 13,
-        out_specs=[pl.BlockSpec(memory_space=vmem)] * 4,
+        in_specs=[near, rest, near, near, near, rest] + [near] * 7,
+        out_specs=[near] * 3,
         scratch_shapes=[
+            vmem((width, hidden), BF16),
+            vmem((hidden, width), BF16),
+            vmem((4, 1, width), BF16),
+            vmem(brown.shape, BF16),
+            vmem(observed.shape, BF16),
             vmem((rows, width), F32),
             vmem((rows, rows), F32),
             vmem((rows, rows), jnp.int32),
@@ -187,13 +391,65 @@
             vmem((rows, width), F32),
             vmem((8, hidden), F32),
             vmem((8, width), F32),
+            vmem((4, 2, 4, 4, 4) + tile, F32),
+            vmem((2, 4, 4, 2) + tile, F32),
+            vmem((4, 4, 4, 4) + tile, F32),
+            vmem((4, 4, 4, 4) + tile, F32),
+            vmem((4, 4, 2) + tile, F32),
+            vmem((4, 4, 2) + tile, F32),
+            vmem((4, 3, 4, 4) + tile, F32),
+            vmem((4, 3, 4) + tile, F32),
+            vmem((4, 3) + tile, F32),
+            vmem((3, 4, 2) + tile, F32),
+            vmem((3, 2) + tile, F32),
+            vmem((4, 2) + tile, F32),
+            vmem((6,) + tile, F32),
+            dma((6,)), dma((6,)), dma((4,)), dma((4,)), dma((6,)), dma((6,)), dma((5,)),
+            dma((17,)), dma((17,)), dma((45,)), dma((45,)), dma((15,)), dma((15,)), dma((16,)), dma((16,)),
         ],
-        compiler_params=pltpu.CompilerParams(vmem_limit_bytes=58 * 1024 * 1024),
-        name="solve",
+        compiler_params=pltpu.CompilerParams(
+            collective_id=0, has_side_effects=True, vmem_limit_bytes=58 * 1024 * 1024
+        ),
+        name="whole",
     )(
-        init, brown, step.reshape(1, -1), length.reshape(1, -1), obs, observed, w_in,
+        init, brown, step.reshape(1, -1), length.reshape(1, -1), obs.T, observed, w_in,
         b_in.reshape(1, -1), w_out, b_out.reshape(1, -1), dec, prior.reshape(1, -1), diff.reshape(1, -1),
     )
+
+
+def finish_kernel(elbo_in, out, ginit_in, elbo, w_in, w_out, dec, b_in, b_out, scores, ginit):
+    me = lax.axis_index("mp")
+
+    def gathered(u):
+        return out[:, :, :, u].reshape(256, 128)
+
+    elbo[...] = elbo_in[...]
+    ginit[...] = ginit_in[...]
+    w_in[:, :128] = gathered(0)
+    w_in[:, 128:] = gathered(1)
+    w_out[:128, :] = gathered(2).T
+    w_out[128:, :] = gathered(3).T
+    dec[...] = gathered(4)
+    for r in range(2):
+        b_in[:, r * 128 : (r + 1) * 128] = out[0, 0, 0, 5, pl.ds(2 * me + r, 1), :]
+        b_out[:, r * 128 : (r + 1) * 128] = out[0, 0, 1, 5, r : r + 1, :]
+    first = lax.broadcasted_iota(jnp.int32, (1, 128), 1) == 0
+    both = jnp.where(first, out[0, 0, 1, 5, 2:3, :], out[0, 0, 1, 5, 3:4, :])
+    scores[...] = both[:, :2]
+
+
+def unpack(elbo, out, ginit):
+    vmem = pltpu.VMEM
+    return pl.pallas_call(
+        finish_kernel,
+        out_shape=tuple(
+            jax.ShapeDtypeStruct(s, F32)
+            for s in ((1, 128), (256, 256), (256, 256), (256, 128), (1, 256), (1, 256), (1, 2), (128, 256))
+        ),
+        in_specs=[pl.BlockSpec(memory_space=vmem)] * 3,
+        out_specs=[pl.BlockSpec(memory_space=vmem)] * 8,
+        name="unpack",
+    )(elbo, out, ginit)
 
 
 def on_device(
@@ -201,25 +457,14 @@
     w_in, b_in, w_out, b_out, decoder, prior_rate, diffusion,
 ):
     total = init_state.shape[0] * lax.axis_size(BATCH_MP)
-    share = w_in.shape[1]
-    w_in_all = lax.all_gather(w_in, "mp", axis=1, tiled=True)
-    w_out_all = lax.all_gather(w_out, "mp", axis=0, tiled=True)
-    b_in_all = lax.all_gather(b_in, "mp", axis=0, tiled=True)
-    elbo, big, small, grad_init = solve(
+    elbo, parts, grad_init = whole(
         total, init_state, brownian, step_size, lengths, obs_steps, observed,
-        w_in_all, b_in_all, w_out_all, b_out, decoder, prior_rate, diffusion,
-    )
-    big, small = lax.psum((big, small), BATCH_MP)
-    me = lax.axis_index("mp")
-    own = lax.dynamic_index_in_dim(big, me, 2, keepdims=False)
-    own = own.reshape(2, 2, 256, 128)
-    own_in = jnp.concatenate([own[0, 0], own[0, 1]], axis=1)
-    own_out = jnp.concatenate([own[1, 0], own[1, 1]], axis=1).T
-    grad_dec = small[:, :, :, 0].reshape(256, 128)
-    own_b = lax.dynamic_slice_in_dim(small[0, 0, 0, 1].reshape(-1), me * share, share, 0)
-    tail = small[0, 0, 1, 1]
+        w_in, b_in, w_out, b_out, decoder, prior_rate, diffusion,
+    )
+    elbo, own_in, own_out, grad_dec, own_b, grad_b_out, scores, grad_init = unpack(elbo, parts, grad_init)
     return (
-        elbo.reshape(-1), tail[2:4, 0], own_in, own_b, own_out, tail[0:2].reshape(-1), grad_dec, grad_init,
+        elbo.reshape(-1), scores.reshape(-1), own_in, own_b.reshape(-1), own_out, grad_b_out.reshape(-1),
+        grad_dec, grad_init,
     )
 
 

time: 253 us -> 86.6 us (0.34)
  waiting for transfers between devices: 160 us -> 0 us
  Pallas kernels: 37.7 us -> 84.6 us
  blocking collectives: 31.6 us -> 0 us
  between operations: 14.1 us -> 0.64 us
  local copies, waits for them, and re-layouts: 8.79 us -> 1.22 us
    psum x1 -> x0, waiting for transfers between devices: 160 us -> none  [on_device(): big, small = lax.psum((big, small), BATCH_MP)]
    pallas_call x1 -> x2, Pallas kernels: 37.7 us -> 84.6 us  [the longest x1 82.5 us: whole(): pl.pallas_call(functools.partial(whole_kernel, 1.0 / total), out_shape=(j...]
    all_gather x3 -> x0, blocking collectives: 31.6 us -> none  [the longest x1 13 us: on_device(): w_in_all = lax.all_gather(w_in, 'mp', axis=1, tiled=True)]
    unnamed x3 -> x0, local copies, waits for them, and re-layouts: 2.91 us -> none
  transfers between devices with their start and end apart: 1 -> 0, of which waited for: 1 -> 0; matrix products, arithmetic and copies ran while one was open for 0% -> 0% of each run, Pallas kernels for 0% -> 0%
where the time goes in v3:
time: 86.6 us; the launch traced here: 86.4 us
  Pallas kernels  84.6 us (98%)
  local copies, waits for them, and re-layouts  1.22 us (1%)
    pallas_call x1, Pallas kernels, whole(): pl.pallas_call(functools.partial(whole_kernel, 1.0 / total), out_shape=(j...  82.5 us
    pallas_call x1, Pallas kernels, unpack(): pl.pallas_call(finish_kernel, out_shape=tuple((jax.ShapeDtypeStruct(s, F3...  2.1 us

profile of v3, /device:TPU:1, one launch (start us, length us, event | category | flops | bytes accessed | tf_op | source)
XLA Modules:
  0.0 86.4 jit_solution(13700047133950528520)
XLA Ops:
  0.6 1.2 %reshape.48.b_in = bf16[1,256]{1,0:T(2,128)(2,1)} reshape(bf16[256]{0:T(256)(128)(2,1)} %param.20) | data formatting | bytes 1024 | tf_op jit(solution)/shard_map/reshape | solution.py:416
  1.9 82.5 %whole.1 = (f32[1,128]{1,0:T(1,128)}, f32[2,4,4,6,8,128]{5,4,3,2,1,0:T(8,128)}, f32[128,256]{1,0:T(8,128)}) custom-call(f32[128,256]{1,0:T(8,128)} %init.1, bf16[32,128,256]{2,1,0:T(8,128)(2,1)} %brown_hbm.1, f32[1,128]{1,0:T(1,128)} %bitcast.14, s32[1,128]{1,0:T(1,128)} %bitcast.15, s32[8,128]{1,0:T(8,128)} %bitcast.10, bf16[128,8,128]{2,1,0:T(8,128)(2,1)} %observed_hbm.1, ...), custom_call_target="tpu_custom_call" | custom-call | tf_op jit(solution)/shard_map/whole/pallas_call | solution.py:359
  84.3 2.1 %unpack.1 = (f32[1,128]{1,0:T(1,128)}, f32[256,256]{1,0:T(8,128)}, f32[256,256]{1,0:T(8,128)}, f32[256,128]{1,0:T(8,128)}, f32[1,256]{1,0:T(1,128)}, /*index=5*/...) custom-call(f32[1,128]{1,0:T(1,128)} %get-tuple-element.19.elbo_in, f32[2,4,4,6,8,128]{5,4,3,2,1,0:T(8,128)} %get-tuple-element.20.out, ...), custom_call_target="tpu_custom_call" | custom-call | tf_op jit(solution)/shard_map/unpack/pallas_call | solution.py:443

commit v4 on v3

--- a/solution.py
+++ b/solution.py
@@ -1,4 +1,5 @@
 import functools
+import itertools
 
 import jax
 import jax.numpy as jnp
@@ -10,7 +11,7 @@
 
 BATCH_MP = ("batch_0", "batch_1", "batch_2", "mp")
 F32, BF16 = jnp.float32, jnp.bfloat16
-UNROLL = 2
+UNROLL = 4
 
 
 def mm(a, b):
@@ -23,7 +24,19 @@
 
 AXES = {"x": "mp", "y": "batch_0", "z": "batch_1", "c": "batch_2"}
 LOGICAL = pl.DeviceIdType.MESH
-ORDERS = ("xyz", "xyz", "yzx", "zxy")
+FIRST = "xxyz"
+COPIES = 144
+
+
+def pack(tiles):
+    rows, marks = [], []
+    for tile in tiles:
+        top = jnp.max(jnp.max(jnp.abs(tile), axis=0, keepdims=True), axis=1, keepdims=True)
+        power = jnp.ceil(jnp.log2(jnp.maximum(top, 1e-30) * (1.0 / 32000.0)))
+        rows.append(jnp.floor(tile * jnp.exp2(-power) + 0.5))
+        marks.append(jnp.broadcast_to(power, (1, 128)))
+    marks.append(jnp.zeros((3, 128), F32))
+    return jnp.concatenate(rows + marks, axis=0).astype(jnp.int32).astype(jnp.int16)
 
 
 def far(axis, where):
@@ -48,13 +61,12 @@
 def whole_kernel(
     scale,
     init, brown_hbm, step, length, obs, observed_hbm, w_in, b_in, w_out, b_out, dec, prior, diff,
-    elbo, out, ginit,
+    elbo, out, tiny_out, ginit,
     wi, wo, bi, brown, observed,
     state, stepb, lenb, dr, obsb, obsf, acc, klacc, traj_t, acts, scaled, pre, back, upd_t,
-    w_in_t, w_out_t, dec_t, cot, sum_in, sum_out,
-    big, small, got, cur, small_got, small_cur, r1, r2, r3, s1, s2, sx, fin,
-    wsend, wrecv, bsend, brecv, psend, precv, local,
-    dsend, drecv, send, recv, gsend, grecv, hsend, hrecv,
+    w_in_t, w_out_t, dec_t, cot, ob, sum_in, sum_out,
+    big, small, tiny, got, cur, mid, r1, r2, small_got, small_cur, s1, s2, tiny_got, tiny_cur, t1, t2, packed,
+    wsend, wrecv, bsend, brecv, psend, precv, local, send, recv,
 ):
     steps, rows, width = brown.shape
     hidden = wi.shape[1]
@@ -75,10 +87,12 @@
 
     plane = [(dy, dz) for dy in range(4) for dz in range(4) if (dy, dz) != (0, 0)]
 
-    def in_plane(dy, dz):
-        return {AXES["y"]: other("y", dy), AXES["z"]: other("z", dz)}
-
-    meet([mate] + [far("x", other("x", d)) for d in (1, 2, 3)] + [in_plane(*p) for p in plane])
+    def in_plane(axes, da, db):
+        return {AXES[axes[0]]: other(axes[0], da), AXES[axes[1]]: other(axes[1], db)}
+
+    peers = [far(a, other(a, d)) for a in "xyz" for d in (1, 2, 3)]
+    peers += [in_plane(axes, *p) for axes in ("yz", "xz", "xy") for p in plane if 0 not in p]
+    meet([mate] + peers)
 
     right, left, across = other("x", 1), other("x", 3), other("x", 2)
     depth, share = w_in.shape
@@ -97,13 +111,14 @@
     out_l = remote(own_out, at_out(me), wsend.at[1], wrecv.at[1], to_left)
     out_r = remote(own_out, at_out(me), wsend.at[2], wrecv.at[2], to_right)
     in_l = remote(own_in, at_in(me), wsend.at[3], wrecv.at[3], to_left)
+    own_bias = bi.at[pl.ds(pl.multiple_of(me * share, share), share)]
     biases = [
-        remote(b_in, bi.at[me], bsend.at[d], brecv.at[d], far("x", other("x", d))) for d in (1, 2, 3)
+        remote(b_in, own_bias, bsend.at[d], brecv.at[d], far("x", other("x", d))) for d in (1, 2, 3)
     ]
     kept = [
         pltpu.make_async_copy(w_in, wi.at[:, pl.ds(pl.multiple_of(me * share, share), share)], local.at[0]),
         pltpu.make_async_copy(w_out, wo.at[pl.ds(pl.multiple_of(me * share, share), share), :], local.at[1]),
-        pltpu.make_async_copy(b_in, bi.at[me], local.at[2]),
+        pltpu.make_async_copy(b_in, own_bias, local.at[2]),
     ]
     for copy in kept:
         copy.start()
@@ -119,7 +134,7 @@
     acc[...] = jnp.zeros_like(acc)
     sum_in[...] = jnp.zeros_like(sum_in)
     sum_out[...] = jnp.zeros_like(sum_out)
-    small[...] = jnp.zeros_like(small)
+    tiny[...] = jnp.zeros_like(tiny)
     state[...] = init[...]
     inv = 1.0 / diff[...]
     loads[0].wait()
@@ -153,7 +168,7 @@
 
     w_in_t[...] = wi[...].T
     w_out_t[...] = wo[...].T
-    bias = jnp.concatenate([bi[m] for m in range(4)], axis=1).astype(F32)
+    bias = bi[...].astype(F32).reshape(1, hidden)
     loads[1].wait()
 
     def see(k, rounded):
@@ -211,6 +226,9 @@
     final = gathered(steps)
     back[at(steps), :] = final
     cot[...] = mm(final, dec_t[...])
+    final = gathered(steps - 1)
+    back[at(steps - 1), :] = final
+    ob[...] = mm(final, dec_t[...])
 
     def backward(i, carry):
         k = steps - 1 - i
@@ -222,12 +240,13 @@
         value = acts[at(k), :].astype(F32)
         pre_grad = mm(rounded, w_out_t[...]) * (1.0 - value * value)
         pre_round = pre_grad.astype(BF16)
-        seen = gathered(k)
-        cot[...] = (
-            c + factor * prior[...] * part + (mm(pre_round, w_in_t[...]) + mm(seen, dec_t[...]))
-        )
+        ahead = ob[...]
+        before = jnp.maximum(k - 1, 0)
+        seen = gathered(before)
+        ob[...] = mm(seen, dec_t[...])
+        cot[...] = (c + factor * prior[...] * part + ahead) + mm(pre_round, w_in_t[...])
         pre[at(k), :] = pre_round
-        back[at(k), :] = seen
+        back[at(before), :] = seen
         upd_t[:, at(k)] = rounded.T
         sum_in[...] += jnp.sum(pre_grad.reshape(rows // 8, 8, hidden), axis=0)
         sum_out[...] += jnp.sum(update.reshape(rows // 8, 8, width), axis=0)
@@ -239,114 +258,129 @@
     pending = []
     first = {}
     flying = {}
-
-    def pick(ref, dims, axis, index):
-        return ref.at[tuple(index if a == axis else slice(None) for a in dims)]
-
-    def hop(flow, stage, d, src, box, axis):
-        n = (flow * 3 + stage) * 3 + d - 1
-        copy = remote(src, box.at[d - 1], send.at[n], recv.at[n], far(axis, other(axis, d)))
+    used = itertools.count()
+
+    def go(src, dst, to, *key):
+        n = next(used)
+        copy = remote(src, dst, send.at[n], recv.at[n], to)
         pending.append(copy)
-        flying.setdefault((flow, stage), []).append(copy)
-
-    def start(flow, stage, ref, dims, axis, box):
-        for d in (2, 1, 3):
-            hop(flow, stage, d, pick(ref, dims, axis, other(axis, d)), box, axis)
-
-    def finish(flow, stage, ref, dims, axis, box):
-        for copy in flying[flow, stage]:
+        flying.setdefault(key, []).append(copy)
+
+    def landed(*key):
+        for copy in flying[key]:
             copy.wait_recv()
-        mine = pick(ref, dims, axis, place[axis])[...]
-        return mine + box[0] + box[1] + box[2]
-
-    def to_mate(n, src, dst):
-        copy = remote(src, dst, dsend.at[n], drecv.at[n], mate)
-        pending.append(copy)
-        return copy
+
+    def along(dims, axis, index):
+        return tuple(index if a == axis else slice(None) for a in dims)
 
     def grads(d, base, left_ref, right_ref):
         n = other("x", d)
         cols = pl.ds(pl.multiple_of(n * width, width), width)
         grad = mm(left_ref[:, : steps * rows], right_ref[:, cols]) * scale
-        for h in range(2):
-            u = base + h
+        for u in (base, base + 1):
+            h = u - base
             big[u, :, n] = grad[:, h * rows : (h + 1) * rows].reshape(2, 4, 4, 8, rows)
-        for h in range(2):
-            u = base + h
-            first[u, d] = to_mate(u * 4 + d, big.at[u, 1 - core, n], got.at[u, n])
+        for u in (base, base + 1):
+            go(big.at[u, 1 - core, n], got.at[u, n], mate, "half", u, d)
 
     for d in (2, 1, 3, 0):
         grads(d, 0, traj_t, pre)
 
     grad_dec = mm(traj_t[...], back[...]) * scale
-    small[:, :, :, 0] = (grad_dec[:, :rows] + grad_dec[:, rows:]).reshape(2, 4, 4, 8, rows)
+    small[...] = (grad_dec[:, :rows] + grad_dec[:, rows:]).reshape(2, 4, 4, 8, rows)
     row_in = jnp.sum(sum_in[...], axis=0, keepdims=True) * scale
     row_out = jnp.sum(sum_out[...], axis=0, keepdims=True) * scale
     for r in range(hidden // rows):
-        small[0, 0, 0, 1, r : r + 1, :] = row_in[:, r * rows : (r + 1) * rows]
+        tiny[0, r : r + 1, :] = row_in[:, r * rows : (r + 1) * rows]
     for r in range(width // rows):
-        small[0, 0, 1, 1, r : r + 1, :] = row_out[:, r * rows : (r + 1) * rows]
+        tiny[1, r : r + 1, :] = row_out[:, r * rows : (r + 1) * rows]
     for r, part in ((2, loglik), (3, klacc[...])):
         total = jnp.sum(jnp.sum(part, axis=0, keepdims=True), axis=1, keepdims=True) * scale
-        small[0, 0, 1, 1, r : r + 1, :] = jnp.broadcast_to(total, (1, rows))
-    first[4] = to_mate(16, small.at[1 - core], small_got)
+        tiny[1, r : r + 1, :] = jnp.broadcast_to(total, (1, rows))
+    go(small.at[1 - core], small_got, mate, "half", "small")
+    go(tiny.at[1 - core], tiny_got, mate, "half", "tiny")
 
     for d in (2, 1, 3, 0):
         grads(d, 2, upd_t, acts)
         n = other("x", d)
         for u in (0, 1):
-            first[u, d].wait_recv()
+            landed("half", u, d)
             cur[u, n] = big[u, core, n] + got[u, n]
             if d:
-                hop(u, 0, d, cur.at[u, n], r1.at[u], "x")
-    first[4].wait_recv()
+                go(cur.at[u, n], r1.at[u, d - 1], far("x", n), "one", u)
+
+    landed("half", "small")
     small_cur[...] = small[core] + small_got[...]
-    start(4, 0, small_cur, "yz", "y", s1)
+    landed("half", "tiny")
+    tiny_cur[0] = tiny[core] + tiny_got[...]
+    for d in (2, 1, 3):
+        to = far("y", other("y", d))
+        go(small_cur.at[other("y", d)], s1.at[d - 1], to, "one", "small")
+        go(tiny_cur.at[0], t1.at[place["y"]], to, "one", "tiny")
     for u in (2, 3):
+        axis = FIRST[u]
         for d in (2, 1, 3, 0):
-            first[u, d].wait_recv()
+            landed("half", u, d)
         cur[u] = big[u, core] + got[u]
-        start(u, 0, cur.at[u], "xyz", ORDERS[u][0], r1.at[u])
-
-    small_got[0] = finish(4, 0, small_cur, "yz", "y", s1)
-    start(4, 1, small_got.at[0], "z", "z", s2)
-    for u in (0, 1, 2, 3):
-        axis = ORDERS[u][0]
-        got[u, 0] = finish(u, 0, cur.at[u], "xyz", axis, r1.at[u])
-        dims = "xyz".replace(axis, "")
-        start(u, 1, got.at[u, 0], dims, ORDERS[u][1], r2.at[u])
-    s = finish(4, 1, small_got.at[0], "z", "z", s2)
-    small_got[1, 0] = s
-    for d in (1, 2, 3):
-        n = (4 * 3 + 2) * 3 + d - 1
-        copy = remote(small_got.at[1, 0], sx.at[me], send.at[n], recv.at[n], far("x", other("x", d)))
-        pending.append(copy)
-        flying.setdefault((4, 2), []).append(copy)
-    sx[me] = s
-    for u in (0, 1, 2, 3):
-        axis = ORDERS[u][1]
-        dims = "xyz".replace(ORDERS[u][0], "")
-        got[u, 1, 0] = finish(u, 1, got.at[u, 0], dims, axis, r2.at[u])
-        start(u, 2, got.at[u, 1, 0], ORDERS[u][2], ORDERS[u][2], r3.at[u])
-    for copy in flying[4, 2]:
-        copy.wait_recv()
-    fin[4:6] = sx[0] + sx[1] + sx[2] + sx[3]
-    for u in (0, 1, 2, 3):
-        fin[u] = finish(u, 2, got.at[u, 1, 0], ORDERS[u][2], ORDERS[u][2], r3.at[u])
+        for d in (2, 1, 3):
+            p = other(axis, d)
+            go(cur.at[u].at[along("xyz", axis, p)], r1.at[u, d - 1], far(axis, p), "one", u)
+
+    landed("one", "tiny")
+    t1[place["y"]] = tiny_cur[0]
+    tiny_cur[1] = t1[0] + t1[1] + t1[2] + t1[3]
+    landed("one", "small")
+    small_got[0] = small_cur[place["y"]] + s1[0] + s1[1] + s1[2]
+    for dx, dz in plane:
+        to = in_plane("xz", dx, dz)
+        go(small_got.at[0, other("z", dz)], s2.at[me, place["z"]], to, "two", "small")
+        go(tiny_cur.at[1], t2.at[me, place["z"]], to, "two", "tiny")
+    for flow, members in (("x", (0, 1)), ("y", (2,)), ("z", (3,))):
+        for u in members:
+            landed("one", u)
+            own = cur[(u,) + along("xyz", flow, place[flow])]
+            mid[u] = own + r1[u, 0] + r1[u, 1] + r1[u, 2]
+        axes = "xyz".replace(flow, "")
+        us = pl.ds(members[0], len(members))
+        for n, (da, db) in enumerate(plane):
+            src = mid.at[us, other(axes[0], da), other(axes[1], db)]
+            go(src, r2.at[n, us], in_plane(axes, da, db), "two", flow)
+
+    def summed(parts):
+        total = parts[0]
+        for part in parts[1:]:
+            total = total + part
+        return total
+
+    landed("two", "small")
+    s2[me, place["z"]] = small_got[0, place["z"]]
+    landed("two", "tiny")
+    t2[me, place["z"]] = tiny_cur[1]
+    tiny_out[core] = summed([t2[x, z] for x in range(4) for z in range(4)])
+    go(tiny_out.at[core], tiny_out.at[core], mate, "last", "tiny")
+    tiles = {4: summed([s2[x, z] for x in range(4) for z in range(4)])}
+    for flow, members in (("y", (2,)), ("z", (3,)), ("x", (0, 1))):
+        landed("two", flow)
+        axes = "xyz".replace(flow, "")
+        for u in members:
+            own = mid[u, place[axes[0]], place[axes[1]]]
+            tiles[u] = summed([own] + [r2[n, u] for n in range(15)])
+    packed[...] = pack([tiles[t] for t in range(5)])
 
     home = out.at[core, place["y"], place["z"]]
-    spread = []
     for n, (dy, dz) in enumerate(plane):
-        spread.append(remote(fin, home, gsend.at[n], grecv.at[n], in_plane(dy, dz)))
-    pair = [remote(fin, home, hsend.at[15], hrecv.at[15], mate)]
-    out[core, place["y"], place["z"]] = fin[...]
+        go(packed, home, in_plane("yz", dy, dz), "all", n)
+    go(packed, home, mate, "last", "own")
+    out[core, place["y"], place["z"]] = packed[...]
     for n, (dy, dz) in enumerate(plane):
-        spread[n].wait_recv()
+        landed("all", n)
         came = out.at[core, lax.rem(place["y"] + 4 - dy, 4), lax.rem(place["z"] + 4 - dz, 4)]
-        pair.append(remote(came, came, hsend.at[n], hrecv.at[n], mate))
-    for copy in pair:
-        copy.wait()
-    for copy in pending + spread:
+        go(came, came, mate, "last", n)
+    landed("last", "tiny")
+    landed("last", "own")
+    for n in range(len(plane)):
+        landed("last", n)
+    for copy in pending:
         copy.wait_send()
 
 
@@ -360,15 +394,16 @@
         functools.partial(whole_kernel, 1.0 / total),
         out_shape=(
             jax.ShapeDtypeStruct((1, rows), F32),
-            jax.ShapeDtypeStruct((2, 4, 4, 6) + tile, F32),
+            jax.ShapeDtypeStruct((2, 4, 4, 48, 128), jnp.int16),
+            jax.ShapeDtypeStruct((2,) + tile, F32),
             jax.ShapeDtypeStruct((rows, width), F32),
         ),
         in_specs=[near, rest, near, near, near, rest] + [near] * 7,
-        out_specs=[near] * 3,
+        out_specs=[near] * 4,
         scratch_shapes=[
             vmem((width, hidden), BF16),
             vmem((hidden, width), BF16),
-            vmem((4, 1, width), BF16),
+            vmem((hidden,), BF16),
             vmem(brown.shape, BF16),
             vmem(observed.shape, BF16),
             vmem((rows, width), F32),
@@ -389,23 +424,28 @@
             vmem((width, hidden), BF16),
             vmem((width, width), BF16),
             vmem((rows, width), F32),
+            vmem((rows, width), F32),
             vmem((8, hidden), F32),
             vmem((8, width), F32),
             vmem((4, 2, 4, 4, 4) + tile, F32),
-            vmem((2, 4, 4, 2) + tile, F32),
+            vmem((2, 4, 4) + tile, F32),
+            vmem((2,) + tile, F32),
             vmem((4, 4, 4, 4) + tile, F32),
             vmem((4, 4, 4, 4) + tile, F32),
-            vmem((4, 4, 2) + tile, F32),
-            vmem((4, 4, 2) + tile, F32),
+            vmem((4, 4, 4) + tile, F32),
             vmem((4, 3, 4, 4) + tile, F32),
-            vmem((4, 3, 4) + tile, F32),
-            vmem((4, 3) + tile, F32),
-            vmem((3, 4, 2) + tile, F32),
-            vmem((3, 2) + tile, F32),
-            vmem((4, 2) + tile, F32),
-            vmem((6,) + tile, F32),
+            vmem((15, 4) + tile, F32),
+            vmem((4, 4) + tile, F32),
+            vmem((4, 4) + tile, F32),
+            vmem((3, 4) + tile, F32),
+            vmem((4, 4) + tile, F32),
+            vmem(tile, F32),
+            vmem((2,) + tile, F32),
+            vmem((4,) + tile, F32),
+            vmem((4, 4) + tile, F32),
+            vmem((48, 128), jnp.int16),
             dma((6,)), dma((6,)), dma((4,)), dma((4,)), dma((6,)), dma((6,)), dma((5,)),
-            dma((17,)), dma((17,)), dma((45,)), dma((45,)), dma((15,)), dma((15,)), dma((16,)), dma((16,)),
+            dma((COPIES,)), dma((COPIES,)),
         ],
         compiler_params=pltpu.CompilerParams(
             collective_id=0, has_side_effects=True, vmem_limit_bytes=58 * 1024 * 1024
@@ -413,32 +453,33 @@
         name="whole",
     )(
         init, brown, step.reshape(1, -1), length.reshape(1, -1), obs.T, observed, w_in,
-        b_in.reshape(1, -1), w_out, b_out.reshape(1, -1), dec, prior.reshape(1, -1), diff.reshape(1, -1),
-    )
-
-
-def finish_kernel(elbo_in, out, ginit_in, elbo, w_in, w_out, dec, b_in, b_out, scores, ginit):
+        b_in, w_out, b_out.reshape(1, -1), dec, prior.reshape(1, -1), diff.reshape(1, -1),
+    )
+
+
+def finish_kernel(elbo_in, out, tiny, ginit_in, elbo, w_in, w_out, dec, b_in, b_out, scores, ginit, turn):
     me = lax.axis_index("mp")
-
-    def gathered(u):
-        return out[:, :, :, u].reshape(256, 128)
-
     elbo[...] = elbo_in[...]
     ginit[...] = ginit_in[...]
-    w_in[:, :128] = gathered(0)
-    w_in[:, 128:] = gathered(1)
-    w_out[:128, :] = gathered(2).T
-    w_out[128:, :] = gathered(3).T
-    dec[...] = gathered(4)
+    for n in range(32):
+        block = out[n // 16, (n // 4) % 4, n % 4].astype(jnp.int32).astype(F32)
+        rs = slice(n * 8, n * 8 + 8)
+        part = [block[t * 8 : t * 8 + 8] * jnp.exp2(block[40 + t : 41 + t]) for t in range(5)]
+        w_in[rs, :128] = part[0]
+        w_in[rs, 128:] = part[1]
+        turn[rs, :128] = part[2]
+        turn[rs, 128:] = part[3]
+        dec[rs, :] = part[4]
+    w_out[...] = turn[...].T
     for r in range(2):
-        b_in[:, r * 128 : (r + 1) * 128] = out[0, 0, 0, 5, pl.ds(2 * me + r, 1), :]
-        b_out[:, r * 128 : (r + 1) * 128] = out[0, 0, 1, 5, r : r + 1, :]
+        b_in[:, r * 128 : (r + 1) * 128] = tiny[0, pl.ds(2 * me + r, 1), :]
+        b_out[:, r * 128 : (r + 1) * 128] = tiny[1, r : r + 1, :]
     first = lax.broadcasted_iota(jnp.int32, (1, 128), 1) == 0
-    both = jnp.where(first, out[0, 0, 1, 5, 2:3, :], out[0, 0, 1, 5, 3:4, :])
+    both = jnp.where(first, tiny[1, 2:3, :], tiny[1, 3:4, :])
     scores[...] = both[:, :2]
 
 
-def unpack(elbo, out, ginit):
+def unpack(elbo, out, tiny, ginit):
     vmem = pltpu.VMEM
     return pl.pallas_call(
         finish_kernel,
@@ -446,10 +487,11 @@
             jax.ShapeDtypeStruct(s, F32)
             for s in ((1, 128), (256, 256), (256, 256), (256, 128), (1, 256), (1, 256), (1, 2), (128, 256))
         ),
-        in_specs=[pl.BlockSpec(memory_space=vmem)] * 3,
+        in_specs=[pl.BlockSpec(memory_space=vmem)] * 4,
         out_specs=[pl.BlockSpec(memory_space=vmem)] * 8,
+        scratch_shapes=[vmem((256, 256), F32)],
         name="unpack",
-    )(elbo, out, ginit)
+    )(elbo, out, tiny, ginit)
 
 
 def on_device(
@@ -457,11 +499,13 @@
     w_in, b_in, w_out, b_out, decoder, prior_rate, diffusion,
 ):
     total = init_state.shape[0] * lax.axis_size(BATCH_MP)
-    elbo, parts, grad_init = whole(
+    elbo, parts, tiny, grad_init = whole(
         total, init_state, brownian, step_size, lengths, obs_steps, observed,
         w_in, b_in, w_out, b_out, decoder, prior_rate, diffusion,
     )
-    elbo, own_in, own_out, grad_dec, own_b, grad_b_out, scores, grad_init = unpack(elbo, parts, grad_init)
+    elbo, own_in, own_out, grad_dec, own_b, grad_b_out, scores, grad_init = unpack(
+        elbo, parts, tiny, grad_init
+    )
     return (
         elbo.reshape(-1), scores.reshape(-1), own_in, own_b.reshape(-1), own_out, grad_b_out.reshape(-1),
         grad_dec, grad_init,

time: 86.6 us -> 83.7 us (0.967)
  Pallas kernels: 84.6 us -> 82.9 us
  local copies, waits for them, and re-layouts: 1.22 us -> 0 us
    pallas_call x1, Pallas kernels: 82.5 us -> 80.8 us  [whole(): pl.pallas_call(functools.partial(whole_kernel, 1.0 / total), out_shape=(j...]
    reshape x1 -> x0, local copies, waits for them, and re-layouts: 1.22 us -> none  [whole(): b_in.reshape(1, -1)]
where the time goes in v4:
time: 83.7 us; the launch traced here: 83.5 us
  Pallas kernels  82.9 us (99%)
    pallas_call x1, Pallas kernels, whole(): pl.pallas_call(functools.partial(whole_kernel, 1.0 / total), out_shape=(j...  80.8 us
    pallas_call x1, Pallas kernels, unpack(): pl.pallas_call(finish_kernel, out_shape=tuple((jax.ShapeDtypeStruct(s, F3...  2.04 us

profile of v4, /device:TPU:1, one launch (start us, length us, event | category | flops | bytes accessed | tf_op | source)
XLA Modules:
  0.0 83.5 jit_solution(191646379643641615)
XLA Ops:
  0.6 80.8 %whole.1 = (f32[1,128]{1,0:T(1,128)}, s16[2,4,4,48,128]{4,3,2,1,0:T(8,128)(2,1)}, f32[2,8,128]{2,1,0:T(8,128)}, f32[128,256]{1,0:T(8,128)}) custom-call(f32[128,256]{1,0:T(8,128)} %init.1, bf16[32,128,256]{2,1,0:T(8,128)(2,1)} %brown_hbm.1, f32[1,128]{1,0:T(1,128)} %bitcast.14, s32[1,128]{1,0:T(1,128)} %bitcast.15, s32[8,128]{1,0:T(8,128)} %bitcast.10, ...), custom_call_target="tpu_custom_call" | custom-call | tf_op jit(solution)/shard_map/whole/pallas_call | solution.py:393
  81.5 2.0 %unpack.1 = (f32[1,128]{1,0:T(1,128)}, f32[256,256]{1,0:T(8,128)}, f32[256,256]{1,0:T(8,128)}, f32[256,128]{1,0:T(8,128)}, f32[1,256]{1,0:T(1,128)}, /*index=5*/...) custom-call(f32[1,128]{1,0:T(1,128)} %get-tuple-element.20.elbo_in, s16[2,4,4,48,128]{4,3,2,1,0:T(8,128)(2,1)} %get-tuple-element.21.out, ...), custom_call_target="tpu_custom_call" | custom-call | tf_op jit(solution)/shard_map/unpack/pallas_call | solution.py:484

commit v5 on v4

--- a/solution.py
+++ b/solution.py
@@ -24,8 +24,7 @@
 
 AXES = {"x": "mp", "y": "batch_0", "z": "batch_1", "c": "batch_2"}
 LOGICAL = pl.DeviceIdType.MESH
-FIRST = "xxyz"
-COPIES = 144
+COPIES = 168
 
 
 def pack(tiles):
@@ -65,7 +64,7 @@
     wi, wo, bi, brown, observed,
     state, stepb, lenb, dr, obsb, obsf, acc, klacc, traj_t, acts, scaled, pre, back, upd_t,
     w_in_t, w_out_t, dec_t, cot, ob, sum_in, sum_out,
-    big, small, tiny, got, cur, mid, r1, r2, small_got, small_cur, s1, s2, tiny_got, tiny_cur, t1, t2, packed,
+    big, small, tiny, got, cur, mid, r1, chain, r2, small_got, small_cur, s1, s2, tiny_got, tiny_cur, t1, t2, packed,
     wsend, wrecv, bsend, brecv, psend, precv, local, send, recv,
 ):
     steps, rows, width = brown.shape
@@ -85,7 +84,8 @@
     def other(axis, d):
         return lax.rem(place[axis] + d, 4)
 
-    plane = [(dy, dz) for dy in range(4) for dz in range(4) if (dy, dz) != (0, 0)]
+    plane = [(da, db) for da in range(4) for db in range(4) if (da, db) != (0, 0)]
+    plane.sort(key=lambda p: -sum(min(d, 4 - d) for d in p))
 
     def in_plane(axes, da, db):
         return {AXES[axes[0]]: other(axes[0], da), AXES[axes[1]]: other(axes[1], db)}
@@ -283,8 +283,42 @@
         for u in (base, base + 1):
             go(big.at[u, 1 - core, n], got.at[u, n], mate, "half", u, d)
 
-    for d in (2, 1, 3, 0):
-        grads(d, 0, traj_t, pre)
+    def halves(d, base):
+        n = other("x", d)
+        for u in (base, base + 1):
+            landed("half", u, d)
+            cur[u, n] = big[u, core, n] + got[u, n]
+        return n
+
+    def sideways(d):
+        n = halves(d, 2)
+        for e in (2, 1, 3):
+            y, z = other("y", e), other("z", e)
+            go(cur.at[2, n, y], r1.at[2, e - 1, n], far("y", y), "one", 2)
+            go(cur.at[3, n, :, z], r1.at[3, e - 1, n], far("z", z), "one", 3)
+
+    def relay(u, block, to):
+        landed("across", u)
+        chain[u, 1] = cur[u, block] + chain[u, 0]
+        go(chain.at[u, 1], chain.at[u, 2], to, "one", u)
+
+    grads(2, 0, traj_t, pre)
+    grads(2, 2, upd_t, acts)
+    grads(1, 2, upd_t, acts)
+    halves(2, 0)
+    go(cur.at[0, across], chain.at[0, 0], to_right, "across", 0)
+    go(cur.at[1, across], chain.at[1, 0], to_left, "across", 1)
+    grads(3, 2, upd_t, acts)
+    sideways(2)
+    grads(0, 2, upd_t, acts)
+    sideways(1)
+    grads(1, 0, traj_t, pre)
+    sideways(3)
+    grads(3, 0, traj_t, pre)
+    sideways(0)
+    grads(0, 0, traj_t, pre)
+    halves(1, 0)
+    go(cur.at[1, right], chain.at[1, 3], to_right, "one", 1)
 
     grad_dec = mm(traj_t[...], back[...]) * scale
     small[...] = (grad_dec[:, :rows] + grad_dec[:, rows:]).reshape(2, 4, 4, 8, rows)
@@ -300,15 +334,11 @@
     go(small.at[1 - core], small_got, mate, "half", "small")
     go(tiny.at[1 - core], tiny_got, mate, "half", "tiny")
 
-    for d in (2, 1, 3, 0):
-        grads(d, 2, upd_t, acts)
-        n = other("x", d)
-        for u in (0, 1):
-            landed("half", u, d)
-            cur[u, n] = big[u, core, n] + got[u, n]
-            if d:
-                go(cur.at[u, n], r1.at[u, d - 1], far("x", n), "one", u)
-
+    halves(3, 0)
+    go(cur.at[0, left], chain.at[0, 3], to_left, "one", 0)
+    relay(0, right, to_right)
+    relay(1, left, to_left)
+    halves(0, 0)
     landed("half", "small")
     small_cur[...] = small[core] + small_got[...]
     landed("half", "tiny")
@@ -317,14 +347,20 @@
         to = far("y", other("y", d))
         go(small_cur.at[other("y", d)], s1.at[d - 1], to, "one", "small")
         go(tiny_cur.at[0], t1.at[place["y"]], to, "one", "tiny")
-    for u in (2, 3):
-        axis = FIRST[u]
-        for d in (2, 1, 3, 0):
-            landed("half", u, d)
-        cur[u] = big[u, core] + got[u]
-        for d in (2, 1, 3):
-            p = other(axis, d)
-            go(cur.at[u].at[along("xyz", axis, p)], r1.at[u, d - 1], far(axis, p), "one", u)
+
+    for flow, members in (("x", (0, 1)), ("y", (2,)), ("z", (3,))):
+        for u in members:
+            landed("one", u)
+            own = cur[(u,) + along("xyz", flow, place[flow])]
+            if flow == "x":
+                mid[u] = own + chain[u, 2] + chain[u, 3]
+            else:
+                mid[u] = own + r1[u, 0] + r1[u, 1] + r1[u, 2]
+        axes = "xyz".replace(flow, "")
+        us = pl.ds(members[0], len(members))
+        for n, (da, db) in enumerate(plane):
+            src = mid.at[us, other(axes[0], da), other(axes[1], db)]
+            go(src, r2.at[n, us], in_plane(axes, da, db), "two", flow)
 
     landed("one", "tiny")
     t1[place["y"]] = tiny_cur[0]
@@ -335,36 +371,26 @@
         to = in_plane("xz", dx, dz)
         go(small_got.at[0, other("z", dz)], s2.at[me, place["z"]], to, "two", "small")
         go(tiny_cur.at[1], t2.at[me, place["z"]], to, "two", "tiny")
-    for flow, members in (("x", (0, 1)), ("y", (2,)), ("z", (3,))):
-        for u in members:
-            landed("one", u)
-            own = cur[(u,) + along("xyz", flow, place[flow])]
-            mid[u] = own + r1[u, 0] + r1[u, 1] + r1[u, 2]
-        axes = "xyz".replace(flow, "")
-        us = pl.ds(members[0], len(members))
-        for n, (da, db) in enumerate(plane):
-            src = mid.at[us, other(axes[0], da), other(axes[1], db)]
-            go(src, r2.at[n, us], in_plane(axes, da, db), "two", flow)
-
     def summed(parts):
         total = parts[0]
         for part in parts[1:]:
             total = total + part
         return total
 
+    tiles = {}
+    for flow, members in (("x", (0, 1)), ("y", (2,)), ("z", (3,))):
+        landed("two", flow)
+        axes = "xyz".replace(flow, "")
+        for u in members:
+            own = mid[u, place[axes[0]], place[axes[1]]]
+            tiles[u] = summed([own] + [r2[n, u] for n in range(15)])
     landed("two", "small")
     s2[me, place["z"]] = small_got[0, place["z"]]
     landed("two", "tiny")
     t2[me, place["z"]] = tiny_cur[1]
     tiny_out[core] = summed([t2[x, z] for x in range(4) for z in range(4)])
     go(tiny_out.at[core], tiny_out.at[core], mate, "last", "tiny")
-    tiles = {4: summed([s2[x, z] for x in range(4) for z in range(4)])}
-    for flow, members in (("y", (2,)), ("z", (3,)), ("x", (0, 1))):
-        landed("two", flow)
-        axes = "xyz".replace(flow, "")
-        for u in members:
-            own = mid[u, place[axes[0]], place[axes[1]]]
-            tiles[u] = summed([own] + [r2[n, u] for n in range(15)])
+    tiles[4] = summed([s2[x, z] for x in range(4) for z in range(4)])
     packed[...] = pack([tiles[t] for t in range(5)])
 
     home = out.at[core, place["y"], place["z"]]
@@ -372,7 +398,7 @@
         go(packed, home, in_plane("yz", dy, dz), "all", n)
     go(packed, home, mate, "last", "own")
     out[core, place["y"], place["z"]] = packed[...]
-    for n, (dy, dz) in enumerate(plane):
+    for n, (dy, dz) in reversed(list(enumerate(plane))):
         landed("all", n)
         came = out.at[core, lax.rem(place["y"] + 4 - dy, 4), lax.rem(place["z"] + 4 - dz, 4)]
         go(came, came, mate, "last", n)
@@ -434,6 +460,7 @@
             vmem((4, 4, 4, 4) + tile, F32),
             vmem((4, 4, 4) + tile, F32),
             vmem((4, 3, 4, 4) + tile, F32),
+            vmem((2, 4, 4, 4) + tile, F32),
             vmem((15, 4) + tile, F32),
             vmem((4, 4) + tile, F32),
             vmem((4, 4) + tile, F32),

time: 83.7 us -> 80.7 us (0.964)
  Pallas kernels: 82.9 us -> 79.9 us
    pallas_call x1, Pallas kernels: 80.8 us -> 77.8 us  [whole(): pl.pallas_call(functools.partial(whole_kernel, 1.0 / total), out_shape=(j...]
where the time goes in v5:
time: 80.7 us; the launch traced here: 80.5 us
  Pallas kernels  79.9 us (99%)
    pallas_call x1, Pallas kernels, whole(): pl.pallas_call(functools.partial(whole_kernel, 1.0 / total), out_shape=(j...  77.8 us
    pallas_call x1, Pallas kernels, unpack(): pl.pallas_call(finish_kernel, out_shape=tuple((jax.ShapeDtypeStruct(s, F3...  2.04 us

profile of v5, /device:TPU:1, one launch (start us, length us, event | category | flops | bytes accessed | tf_op | source)
XLA Modules:
  0.0 80.5 jit_solution(10320343078755469705)
XLA Ops:
  0.6 77.8 %whole.1 = (f32[1,128]{1,0:T(1,128)}, s16[2,4,4,48,128]{4,3,2,1,0:T(8,128)(2,1)}, f32[2,8,128]{2,1,0:T(8,128)}, f32[128,256]{1,0:T(8,128)}) custom-call(f32[128,256]{1,0:T(8,128)} %init.1, bf16[32,128,256]{2,1,0:T(8,128)(2,1)} %brown_hbm.1, f32[1,128]{1,0:T(1,128)} %bitcast.14, s32[1,128]{1,0:T(1,128)} %bitcast.15, s32[8,128]{1,0:T(8,128)} %bitcast.10, ...), custom_call_target="tpu_custom_call" | custom-call | tf_op jit(solution)/shard_map/whole/pallas_call | solution.py:419
  78.5 2.0 %unpack.1 = (f32[1,128]{1,0:T(1,128)}, f32[256,256]{1,0:T(8,128)}, f32[256,256]{1,0:T(8,128)}, f32[256,128]{1,0:T(8,128)}, f32[1,256]{1,0:T(1,128)}, /*index=5*/...) custom-call(f32[1,128]{1,0:T(1,128)} %get-tuple-element.20.elbo_in, s16[2,4,4,48,128]{4,3,2,1,0:T(8,128)(2,1)} %get-tuple-element.21.out, ...), custom_call_target="tpu_custom_call" | custom-call | tf_op jit(solution)/shard_map/unpack/pallas_call | solution.py:511

commit v6 on v5

--- a/solution.py
+++ b/solution.py
@@ -11,7 +11,7 @@
 
 BATCH_MP = ("batch_0", "batch_1", "batch_2", "mp")
 F32, BF16 = jnp.float32, jnp.bfloat16
-UNROLL = 4
+UNROLL = 8
 
 
 def mm(a, b):
@@ -59,9 +59,9 @@
 
 def whole_kernel(
     scale,
-    init, brown_hbm, step, length, obs, observed_hbm, w_in, b_in, w_out, b_out, dec, prior, diff,
+    init_in, brown_in, step_in, length_in, obs_in, observed_in, w_in, b_in, w_out, b_out_in, dec_in, prior_in, diff_in,
     elbo, out, tiny_out, ginit,
-    wi, wo, bi, brown, observed,
+    wi, wo, bi, init, brown, step, length, obs, observed, b_out, dec, prior, diff,
     state, stepb, lenb, dr, obsb, obsf, acc, klacc, traj_t, acts, scaled, pre, back, upd_t,
     w_in_t, w_out_t, dec_t, cot, ob, sum_in, sum_out,
     big, small, tiny, got, cur, mid, r1, chain, r2, small_got, small_cur, s1, s2, tiny_got, tiny_cur, t1, t2, packed,
@@ -70,15 +70,32 @@
     steps, rows, width = brown.shape
     hidden = wi.shape[1]
     n_obs = obs.shape[0]
-    loads = [
-        pltpu.make_async_copy(observed_hbm, observed, local.at[3]),
-        pltpu.make_async_copy(brown_hbm, brown, local.at[4]),
-    ]
-    for copy in loads:
+    loads = []
+
+    def fetch(src, dst):
+        copy = pltpu.make_async_copy(src, dst, local.at[len(loads)])
         copy.start()
+        loads.append(copy)
+
+    me = lax.axis_index("mp")
+    depth, share = w_in.shape
+    own_cols = pl.ds(pl.multiple_of(me * share, share), share)
+    fetch(w_in, wi.at[:, own_cols])
+    fetch(w_out, wo.at[own_cols, :])
+    fetch(b_in, bi.at[own_cols])
+    fetch(step_in, step)
+    fetch(length_in, length)
+    fetch(obs_in, obs)
+    fetch(b_out_in, b_out)
+    fetch(prior_in, prior)
+    fetch(diff_in, diff)
+    fetch(dec_in, dec)
+    fetch(init_in, init)
+    fetch(observed_in, observed)
+    fetch(brown_in, brown)
 
     place = {a: lax.axis_index(AXES[a]) for a in "xyzc"}
-    me, core = place["x"], place["c"]
+    core = place["c"]
     mate = far("c", 1 - core)
 
     def other(axis, d):
@@ -95,7 +112,6 @@
     meet([mate] + peers)
 
     right, left, across = other("x", 1), other("x", 3), other("x", 2)
-    depth, share = w_in.shape
     half = depth // 2
     upper = pl.ds(pl.multiple_of(core * half, half), half)
     to_right, to_left = far("x", right), far("x", left)
@@ -106,22 +122,19 @@
     def at_out(block):
         return wo.at[pl.ds(pl.multiple_of(block * share + core * half, half), half), :]
 
-    own_in, own_out = w_in.at[upper, :], w_out.at[upper, :]
+    for copy in loads[:3]:
+        copy.wait()
+    own_in, own_out = at_in(me), at_out(me)
     in_r = remote(own_in, at_in(me), wsend.at[0], wrecv.at[0], to_right)
     out_l = remote(own_out, at_out(me), wsend.at[1], wrecv.at[1], to_left)
     out_r = remote(own_out, at_out(me), wsend.at[2], wrecv.at[2], to_right)
     in_l = remote(own_in, at_in(me), wsend.at[3], wrecv.at[3], to_left)
-    own_bias = bi.at[pl.ds(pl.multiple_of(me * share, share), share)]
+    own_bias = bi.at[own_cols]
     biases = [
-        remote(b_in, own_bias, bsend.at[d], brecv.at[d], far("x", other("x", d))) for d in (1, 2, 3)
+        remote(own_bias, own_bias, bsend.at[d], brecv.at[d], far("x", other("x", d))) for d in (1, 2, 3)
     ]
-    kept = [
-        pltpu.make_async_copy(w_in, wi.at[:, pl.ds(pl.multiple_of(me * share, share), share)], local.at[0]),
-        pltpu.make_async_copy(w_out, wo.at[pl.ds(pl.multiple_of(me * share, share), share), :], local.at[1]),
-        pltpu.make_async_copy(b_in, own_bias, local.at[2]),
-    ]
-    for copy in kept:
-        copy.start()
+    for copy in loads[3:-1]:
+        copy.wait()
 
     stepb[...] = jnp.broadcast_to(step[...], (rows, rows)).T
     lenb[...] = jnp.broadcast_to(length[...], (rows, rows)).T
@@ -137,7 +150,6 @@
     tiny[...] = jnp.zeros_like(tiny)
     state[...] = init[...]
     inv = 1.0 / diff[...]
-    loads[0].wait()
     obsf[...] = observed[...].astype(F32).reshape(rows * n_obs, dec.shape[1])
 
     sent = []
@@ -159,8 +171,6 @@
     share_with_mate(4, at_in(across))
     out_ll.wait_recv()
     share_with_mate(5, at_out(across))
-    for copy in kept:
-        copy.wait()
     for copy in biases + sent:
         copy.wait()
     for copy in (in_r, out_l, out_r, in_l, in_rr, out_ll):
@@ -169,7 +179,7 @@
     w_in_t[...] = wi[...].T
     w_out_t[...] = wo[...].T
     bias = bi[...].astype(F32).reshape(1, hidden)
-    loads[1].wait()
+    loads[-1].wait()
 
     def see(k, rounded):
         seen = mm(rounded, dec[...])
@@ -370,7 +380,8 @@
     for dx, dz in plane:
         to = in_plane("xz", dx, dz)
         go(small_got.at[0, other("z", dz)], s2.at[me, place["z"]], to, "two", "small")
-        go(tiny_cur.at[1], t2.at[me, place["z"]], to, "two", "tiny")
+    for d in (2, 1, 3):
+        go(tiny_cur.at[1], t2.at[0, place["z"]], far("z", other("z", d)), "two", "tiny")
     def summed(parts):
         total = parts[0]
         for part in parts[1:]:
@@ -387,21 +398,26 @@
     landed("two", "small")
     s2[me, place["z"]] = small_got[0, place["z"]]
     landed("two", "tiny")
-    t2[me, place["z"]] = tiny_cur[1]
-    tiny_out[core] = summed([t2[x, z] for x in range(4) for z in range(4)])
-    go(tiny_out.at[core], tiny_out.at[core], mate, "last", "tiny")
+    t2[0, place["z"]] = tiny_cur[1]
+    tiny_cur[2] = summed([t2[0, z] for z in range(4)])
     tiles[4] = summed([s2[x, z] for x in range(4) for z in range(4)])
     packed[...] = pack([tiles[t] for t in range(5)])
 
     home = out.at[core, place["y"], place["z"]]
     for n, (dy, dz) in enumerate(plane):
         go(packed, home, in_plane("yz", dy, dz), "all", n)
+    for d in (2, 1, 3):
+        go(tiny_cur.at[2], t2.at[1, me], far("x", other("x", d)), "all", "tiny")
     go(packed, home, mate, "last", "own")
     out[core, place["y"], place["z"]] = packed[...]
     for n, (dy, dz) in reversed(list(enumerate(plane))):
         landed("all", n)
         came = out.at[core, lax.rem(place["y"] + 4 - dy, 4), lax.rem(place["z"] + 4 - dz, 4)]
         go(came, came, mate, "last", n)
+    landed("all", "tiny")
+    t2[1, me] = tiny_cur[2]
+    tiny_out[core] = summed([t2[1, x] for x in range(4)])
+    go(tiny_out.at[core], tiny_out.at[core], mate, "last", "tiny")
     landed("last", "tiny")
     landed("last", "own")
     for n in range(len(plane)):
@@ -424,14 +440,22 @@
             jax.ShapeDtypeStruct((2,) + tile, F32),
             jax.ShapeDtypeStruct((rows, width), F32),
         ),
-        in_specs=[near, rest, near, near, near, rest] + [near] * 7,
+        in_specs=[rest] * 13,
         out_specs=[near] * 4,
         scratch_shapes=[
             vmem((width, hidden), BF16),
             vmem((hidden, width), BF16),
             vmem((hidden,), BF16),
+            vmem(init.shape, F32),
             vmem(brown.shape, BF16),
+            vmem((1, rows), F32),
+            vmem((1, rows), jnp.int32),
+            vmem((n_obs, rows), jnp.int32),
             vmem(observed.shape, BF16),
+            vmem((1, width), F32),
+            vmem(dec.shape, BF16),
+            vmem((1, width), F32),
+            vmem((1, width), F32),
             vmem((rows, width), F32),
             vmem((rows, rows), F32),
             vmem((rows, rows), jnp.int32),
@@ -467,11 +491,11 @@
             vmem((3, 4) + tile, F32),
             vmem((4, 4) + tile, F32),
             vmem(tile, F32),
-            vmem((2,) + tile, F32),
+            vmem((3,) + tile, F32),
             vmem((4,) + tile, F32),
-            vmem((4, 4) + tile, F32),
+            vmem((2, 4) + tile, F32),
             vmem((48, 128), jnp.int16),
-            dma((6,)), dma((6,)), dma((4,)), dma((4,)), dma((6,)), dma((6,)), dma((5,)),
+            dma((6,)), dma((6,)), dma((4,)), dma((4,)), dma((6,)), dma((6,)), dma((13,)),
             dma((COPIES,)), dma((COPIES,)),
         ],
         compiler_params=pltpu.CompilerParams(

time: 80.7 us -> 79.1 us (0.980)
  Pallas kernels: 79.9 us -> 78.3 us
    pallas_call x1, Pallas kernels: 77.8 us -> 76.3 us  [whole(): pl.pallas_call(functools.partial(whole_kernel, 1.0 / total), out_shape=(j...]
where the time goes in v6:
time: 79.1 us; the launch traced here: 78.9 us
  Pallas kernels  78.3 us (99%)
    pallas_call x1, Pallas kernels, whole(): pl.pallas_call(functools.partial(whole_kernel, 1.0 / total), out_shape=(j...  76.3 us
    pallas_call x1, Pallas kernels, unpack(): pl.pallas_call(finish_kernel, out_shape=tuple((jax.ShapeDtypeStruct(s, F3...  2.04 us

profile of v6, /device:TPU:1, one launch (start us, length us, event | category | flops | bytes accessed | tf_op | source)
XLA Modules:
  0.0 78.9 jit_solution(8251821196347865773)
XLA Ops:
  0.6 76.3 %whole.1 = (f32[1,128]{1,0:T(1,128)}, s16[2,4,4,48,128]{4,3,2,1,0:T(8,128)(2,1)}, f32[2,8,128]{2,1,0:T(8,128)}, f32[128,256]{1,0:T(8,128)}) custom-call(f32[128,256]{1,0:T(8,128)} %init_in.1, bf16[32,128,256]{2,1,0:T(8,128)(2,1)} %brown_in.1, f32[1,128]{1,0:T(1,128)} %bitcast.14, s32[1,128]{1,0:T(1,128)} %bitcast.15, s32[8,128]{1,0:T(8,128)} %bitcast.10, ...), custom_call_target="tpu_custom_call" | custom-call | tf_op jit(solution)/shard_map/whole/pallas_call | solution.py:435
  76.9 2.0 %unpack.1 = (f32[1,128]{1,0:T(1,128)}, f32[256,256]{1,0:T(8,128)}, f32[256,256]{1,0:T(8,128)}, f32[256,128]{1,0:T(8,128)}, f32[1,256]{1,0:T(1,128)}, /*index=5*/...) custom-call(f32[1,128]{1,0:T(1,128)} %get-tuple-element.20.elbo_in, s16[2,4,4,48,128]{4,3,2,1,0:T(8,128)(2,1)} %get-tuple-element.21.out, ...), custom_call_target="tpu_custom_call" | custom-call | tf_op jit(solution)/shard_map/unpack/pallas_call | solution.py:535

commit v7 on v6

--- a/solution.py
+++ b/solution.py
@@ -113,22 +113,31 @@
 
     right, left, across = other("x", 1), other("x", 3), other("x", 2)
     half = depth // 2
-    upper = pl.ds(pl.multiple_of(core * half, half), half)
     to_right, to_left = far("x", right), far("x", left)
 
-    def at_in(block):
-        return wi.at[upper, pl.ds(pl.multiple_of(block * share, share), share)]
-
-    def at_out(block):
-        return wo.at[pl.ds(pl.multiple_of(block * share + core * half, half), half), :]
+    def at_in(block, part=0, parts=1):
+        size = half // parts
+        at_row = pl.ds(pl.multiple_of(core * half + part * size, size), size)
+        return wi.at[at_row, pl.ds(pl.multiple_of(block * share, share), share)]
+
+    def at_out(block, part=0, parts=1):
+        size = half // parts
+        return wo.at[pl.ds(pl.multiple_of(block * share + core * half + part * size, size), size), :]
+
+    turns = itertools.count()
+
+    def pass_on(ref, to):
+        n = next(turns)
+        return remote(ref, ref, wsend.at[n], wrecv.at[n], to)
 
     for copy in loads[:3]:
         copy.wait()
-    own_in, own_out = at_in(me), at_out(me)
-    in_r = remote(own_in, at_in(me), wsend.at[0], wrecv.at[0], to_right)
-    out_l = remote(own_out, at_out(me), wsend.at[1], wrecv.at[1], to_left)
-    out_r = remote(own_out, at_out(me), wsend.at[2], wrecv.at[2], to_right)
-    in_l = remote(own_in, at_in(me), wsend.at[3], wrecv.at[3], to_left)
+    in_r, out_l = [], []
+    for p in range(2):
+        in_r.append(pass_on(at_in(me, p, 2), to_right))
+        out_l.append(pass_on(at_out(me, p, 2), to_left))
+    out_r = pass_on(at_out(me), to_right)
+    in_l = pass_on(at_in(me), to_left)
     own_bias = bi.at[own_cols]
     biases = [
         remote(own_bias, own_bias, bsend.at[d], brecv.at[d], far("x", other("x", d))) for d in (1, 2, 3)
@@ -154,26 +163,30 @@
 
     sent = []
 
-    def share_with_mate(n, ref):
+    def share_with_mate(ref):
+        n = len(sent)
         sent.append(remote(ref, ref, psend.at[n], precv.at[n], mate))
 
-    in_r.wait_recv()
-    in_rr = remote(at_in(left), at_in(left), wsend.at[4], wrecv.at[4], to_right)
-    share_with_mate(0, at_in(left))
-    out_l.wait_recv()
-    out_ll = remote(at_out(right), at_out(right), wsend.at[5], wrecv.at[5], to_left)
-    share_with_mate(1, at_out(right))
+    in_rr, out_ll = [], []
+    for p in range(2):
+        in_r[p].wait_recv()
+        in_rr.append(pass_on(at_in(left, p, 2), to_right))
+        share_with_mate(at_in(left, p, 2))
+        out_l[p].wait_recv()
+        out_ll.append(pass_on(at_out(right, p, 2), to_left))
+        share_with_mate(at_out(right, p, 2))
     out_r.wait_recv()
-    share_with_mate(2, at_out(left))
+    share_with_mate(at_out(left))
     in_l.wait_recv()
-    share_with_mate(3, at_in(right))
-    in_rr.wait_recv()
-    share_with_mate(4, at_in(across))
-    out_ll.wait_recv()
-    share_with_mate(5, at_out(across))
+    share_with_mate(at_in(right))
+    for p in range(2):
+        in_rr[p].wait_recv()
+        share_with_mate(at_in(across, p, 2))
+        out_ll[p].wait_recv()
+        share_with_mate(at_out(across, p, 2))
     for copy in biases + sent:
         copy.wait()
-    for copy in (in_r, out_l, out_r, in_l, in_rr, out_ll):
+    for copy in in_r + out_l + [out_r, in_l] + in_rr + out_ll:
         copy.wait_send()
 
     w_in_t[...] = wi[...].T
@@ -203,9 +216,7 @@
         residual = (drift + prior[...] * s) * inv
         noise = dr[...] * brown[k].astype(F32)
         state[...] = s + twice(factor) * drift + jnp.where(twice(live), noise, 0.0)
-        scaled[k] = residual * inv
-        square = residual * residual
-        klacc[...] += (0.5 * factor) * (square[:, :rows] + square[:, rows:])
+        scaled[k] = residual
         traj_t[:, at(k)] = rounded.T
         see(k, rounded)
         return carry
@@ -221,9 +232,6 @@
         total = total + misfit * misfit
         acc[j] = misfit.astype(BF16).astype(F32)
     loglik = -0.5 * total
-    divisor = (width * lenb[...] + rows * n_obs).astype(F32)
-    per_series = jnp.sum(loglik - klacc[...], axis=1, keepdims=True) / divisor
-    elbo[...] = per_series.T[0:1, :]
 
     def gathered(k):
         m = jnp.zeros((rows, rows), F32)
@@ -244,7 +252,10 @@
         k = steps - 1 - i
         c = cot[...]
         factor = twice(jnp.where(lenb[...] > k, stepb[...], 0.0))
-        part = scaled[k]
+        residual = scaled[k]
+        square = residual * residual
+        klacc[...] += (0.5 * factor[:, :rows]) * (square[:, :rows] + square[:, rows:])
+        part = residual * inv
         update = factor * (c + part)
         rounded = update.astype(BF16)
         value = acts[at(k), :].astype(F32)
@@ -264,6 +275,9 @@
 
     lax.fori_loop(0, steps, backward, 0, unroll=UNROLL)
     ginit[...] = cot[...]
+    divisor = (width * lenb[...] + rows * n_obs).astype(F32)
+    per_series = jnp.sum(loglik - klacc[...], axis=1, keepdims=True) / divisor
+    elbo[...] = per_series.T[0:1, :]
 
     pending = []
     first = {}
@@ -495,7 +509,7 @@
             vmem((4,) + tile, F32),
             vmem((2, 4) + tile, F32),
             vmem((48, 128), jnp.int16),
-            dma((6,)), dma((6,)), dma((4,)), dma((4,)), dma((6,)), dma((6,)), dma((13,)),
+            dma((10,)), dma((10,)), dma((4,)), dma((4,)), dma((10,)), dma((10,)), dma((13,)),
             dma((COPIES,)), dma((COPIES,)),
         ],
         compiler_params=pltpu.CompilerParams(

time: 79.1 us -> 78.5 us (level)
  no operation moved by 1% of the time
where the time goes in v7:
time: 78.5 us; the launch traced here: 78.3 us
  Pallas kernels  77.7 us (99%)
    pallas_call x1, Pallas kernels, whole(): pl.pallas_call(functools.partial(whole_kernel, 1.0 / total), out_shape=(j...  75.6 us
    pallas_call x1, Pallas kernels, unpack(): pl.pallas_call(finish_kernel, out_shape=tuple((jax.ShapeDtypeStruct(s, F3...  2.04 us

profile of v7, /device:TPU:1, one launch (start us, length us, event | category | flops | bytes accessed | tf_op | source)
XLA Modules:
  0.0 78.3 jit_solution(15537852963853267925)
XLA Ops:
  0.6 75.6 %whole.1 = (f32[1,128]{1,0:T(1,128)}, s16[2,4,4,48,128]{4,3,2,1,0:T(8,128)(2,1)}, f32[2,8,128]{2,1,0:T(8,128)}, f32[128,256]{1,0:T(8,128)}) custom-call(f32[128,256]{1,0:T(8,128)} %init_in.1, bf16[32,128,256]{2,1,0:T(8,128)(2,1)} %brown_in.1, f32[1,128]{1,0:T(1,128)} %bitcast.14, s32[1,128]{1,0:T(1,128)} %bitcast.15, s32[8,128]{1,0:T(8,128)} %bitcast.10, ...), custom_call_target="tpu_custom_call" | custom-call | tf_op jit(solution)/shard_map/whole/pallas_call | solution.py:449
  76.3 2.0 %unpack.1 = (f32[1,128]{1,0:T(1,128)}, f32[256,256]{1,0:T(8,128)}, f32[256,256]{1,0:T(8,128)}, f32[256,128]{1,0:T(8,128)}, f32[1,256]{1,0:T(1,128)}, /*index=5*/...) custom-call(f32[1,128]{1,0:T(1,128)} %get-tuple-element.20.elbo_in, s16[2,4,4,48,128]{4,3,2,1,0:T(8,128)(2,1)} %get-tuple-element.21.out, ...), custom_call_target="tpu_custom_call" | custom-call | tf_op jit(solution)/shard_map/unpack/pallas_call | solution.py:549

commit v8 on v7

--- a/solution.py
+++ b/solution.py
@@ -297,15 +297,25 @@
     def along(dims, axis, index):
         return tuple(index if a == axis else slice(None) for a in dims)
 
-    def grads(d, base, left_ref, right_ref):
+    ready = []
+
+    def flush():
+        for u, d in ready:
+            n = other("x", d)
+            go(big.at[u, 1 - core, n], got.at[u, n], mate, "half", u, d)
+        ready.clear()
+
+    def grads(d, base, left_ref, right_ref, between=()):
         n = other("x", d)
         cols = pl.ds(pl.multiple_of(n * width, width), width)
         grad = mm(left_ref[:, : steps * rows], right_ref[:, cols]) * scale
+        flush()
+        for task in between:
+            task()
         for u in (base, base + 1):
             h = u - base
             big[u, :, n] = grad[:, h * rows : (h + 1) * rows].reshape(2, 4, 4, 8, rows)
-        for u in (base, base + 1):
-            go(big.at[u, 1 - core, n], got.at[u, n], mate, "half", u, d)
+            ready.append((u, d))
 
     def halves(d, base):
         n = other("x", d)
@@ -326,25 +336,24 @@
         chain[u, 1] = cur[u, block] + chain[u, 0]
         go(chain.at[u, 1], chain.at[u, 2], to, "one", u)
 
+    def send_across():
+        halves(2, 0)
+        go(cur.at[0, across], chain.at[0, 0], to_right, "across", 0)
+        go(cur.at[1, across], chain.at[1, 0], to_left, "across", 1)
+
     grads(2, 0, traj_t, pre)
     grads(2, 2, upd_t, acts)
     grads(1, 2, upd_t, acts)
-    halves(2, 0)
-    go(cur.at[0, across], chain.at[0, 0], to_right, "across", 0)
-    go(cur.at[1, across], chain.at[1, 0], to_left, "across", 1)
-    grads(3, 2, upd_t, acts)
-    sideways(2)
-    grads(0, 2, upd_t, acts)
-    sideways(1)
-    grads(1, 0, traj_t, pre)
-    sideways(3)
-    grads(3, 0, traj_t, pre)
-    sideways(0)
-    grads(0, 0, traj_t, pre)
+    grads(3, 2, upd_t, acts, [send_across])
+    grads(0, 2, upd_t, acts, [lambda: sideways(2)])
+    grads(1, 0, traj_t, pre, [lambda: sideways(1)])
+    grads(3, 0, traj_t, pre, [lambda: sideways(3)])
+    grads(0, 0, traj_t, pre, [lambda: sideways(0)])
+    grad_dec = mm(traj_t[...], back[...]) * scale
+    flush()
     halves(1, 0)
     go(cur.at[1, right], chain.at[1, 3], to_right, "one", 1)
 
-    grad_dec = mm(traj_t[...], back[...]) * scale
     small[...] = (grad_dec[:, :rows] + grad_dec[:, rows:]).reshape(2, 4, 4, 8, rows)
     row_in = jnp.sum(sum_in[...], axis=0, keepdims=True) * scale
     row_out = jnp.sum(sum_out[...], axis=0, keepdims=True) * scale

time: 78.5 us -> 77.7 us (0.990)
  Pallas kernels: 77.7 us -> 76.9 us
where the time goes in v8:
time: 77.7 us; the launch traced here: 77.6 us
  Pallas kernels  76.9 us (99%)
    pallas_call x1, Pallas kernels, whole(): pl.pallas_call(functools.partial(whole_kernel, 1.0 / total), out_shape=(j...  74.9 us
    pallas_call x1, Pallas kernels, unpack(): pl.pallas_call(finish_kernel, out_shape=tuple((jax.ShapeDtypeStruct(s, F3...  2.04 us

profile of v8, /device:TPU:1, one launch (start us, length us, event | category | flops | bytes accessed | tf_op | source)
XLA Modules:
  0.0 77.6 jit_solution(15204909152682081252)
XLA Ops:
  0.6 74.9 %whole.1 = (f32[1,128]{1,0:T(1,128)}, s16[2,4,4,48,128]{4,3,2,1,0:T(8,128)(2,1)}, f32[2,8,128]{2,1,0:T(8,128)}, f32[128,256]{1,0:T(8,128)}) custom-call(f32[128,256]{1,0:T(8,128)} %init_in.1, bf16[32,128,256]{2,1,0:T(8,128)(2,1)} %brown_in.1, f32[1,128]{1,0:T(1,128)} %bitcast.14, s32[1,128]{1,0:T(1,128)} %bitcast.15, s32[8,128]{1,0:T(8,128)} %bitcast.10, ...), custom_call_target="tpu_custom_call" | custom-call | tf_op jit(solution)/shard_map/whole/pallas_call | solution.py:458
  75.5 2.0 %unpack.1 = (f32[1,128]{1,0:T(1,128)}, f32[256,256]{1,0:T(8,128)}, f32[256,256]{1,0:T(8,128)}, f32[256,128]{1,0:T(8,128)}, f32[1,256]{1,0:T(1,128)}, /*index=5*/...) custom-call(f32[1,128]{1,0:T(1,128)} %get-tuple-element.20.elbo_in, s16[2,4,4,48,128]{4,3,2,1,0:T(8,128)(2,1)} %get-tuple-element.21.out, ...), custom_call_target="tpu_custom_call" | custom-call | tf_op jit(solution)/shard_map/unpack/pallas_call | solution.py:558

commit v9 on v8

--- a/solution.py
+++ b/solution.py
@@ -11,7 +11,7 @@
 
 BATCH_MP = ("batch_0", "batch_1", "batch_2", "mp")
 F32, BF16 = jnp.float32, jnp.bfloat16
-UNROLL = 8
+UNROLL = 16
 
 
 def mm(a, b):
@@ -203,7 +203,7 @@
         return pl.ds(pl.multiple_of(k * rows, rows), rows)
 
     def forward(k, carry):
-        s = state[...]
+        s = carry
         rounded = s.astype(BF16)
         drift = b_out[...]
         for n in range(0, hidden, width):
@@ -215,13 +215,13 @@
         factor = jnp.where(live, stepb[...], 0.0)
         residual = (drift + prior[...] * s) * inv
         noise = dr[...] * brown[k].astype(F32)
-        state[...] = s + twice(factor) * drift + jnp.where(twice(live), noise, 0.0)
+        following = s + twice(factor) * drift + jnp.where(twice(live), noise, 0.0)
         scaled[k] = residual
         traj_t[:, at(k)] = rounded.T
         see(k, rounded)
-        return carry
-
-    lax.fori_loop(0, steps, forward, 0, unroll=UNROLL)
+        return following
+
+    state[...] = lax.fori_loop(0, steps, forward, state[...], unroll=UNROLL)
     last = state[...].astype(BF16)
     traj_t[:, at(steps)] = last.T
     see(steps, last)

time: 77.7 us -> 77.4 us (level)
  no operation moved by 1% of the time
where the time goes in v9:
time: 77.4 us; the launch traced here: 77.2 us
  Pallas kernels  76.6 us (99%)
    pallas_call x1, Pallas kernels, whole(): pl.pallas_call(functools.partial(whole_kernel, 1.0 / total), out_shape=(j...  74.5 us
    pallas_call x1, Pallas kernels, unpack(): pl.pallas_call(finish_kernel, out_shape=tuple((jax.ShapeDtypeStruct(s, F3...  2.04 us

profile of v9, /device:TPU:1, one launch (start us, length us, event | category | flops | bytes accessed | tf_op | source)
XLA Modules:
  0.0 77.2 jit_solution(1998998091343600499)
XLA Ops:
  0.6 74.5 %whole.1 = (f32[1,128]{1,0:T(1,128)}, s16[2,4,4,48,128]{4,3,2,1,0:T(8,128)(2,1)}, f32[2,8,128]{2,1,0:T(8,128)}, f32[128,256]{1,0:T(8,128)}) custom-call(f32[128,256]{1,0:T(8,128)} %init_in.1, bf16[32,128,256]{2,1,0:T(8,128)(2,1)} %brown_in.1, f32[1,128]{1,0:T(1,128)} %bitcast.14, s32[1,128]{1,0:T(1,128)} %bitcast.15, s32[8,128]{1,0:T(8,128)} %bitcast.10, ...), custom_call_target="tpu_custom_call" | custom-call | tf_op jit(solution)/shard_map/whole/pallas_call | solution.py:458
  75.2 2.0 %unpack.1 = (f32[1,128]{1,0:T(1,128)}, f32[256,256]{1,0:T(8,128)}, f32[256,256]{1,0:T(8,128)}, f32[256,128]{1,0:T(8,128)}, f32[1,256]{1,0:T(1,128)}, /*index=5*/...) custom-call(f32[1,128]{1,0:T(1,128)} %get-tuple-element.20.elbo_in, s16[2,4,4,48,128]{4,3,2,1,0:T(8,128)(2,1)} %get-tuple-element.21.out, ...), custom_call_target="tpu_custom_call" | custom-call | tf_op jit(solution)/shard_map/unpack/pallas_call | solution.py:558
